TPU v7x, 256 devices: a whole 4x4x8 slice. The times are simulated.
256 devices in a mesh: img: 16 (over x, z_lo, core), tp: 16 (over y, z_hi).
Axes of the slice: x: 4, y: 4, z: 8 (z_hi: 4, z_lo: 2; z = z_hi * 2 + z_lo), core: 2. Of those that a mesh axis runs over, the one named last changes fastest.
Arguments:
- patch_tokens: bfloat16 [32768, 1024], P(('img', 'tp')), may hold values from -12 to 12
- norm_gain: float32 [1024], replicated, may hold values from 0.1 to 1.9
- norm_bias: float32 [1024], replicated, may hold values from -3 to 3
- up_weight: bfloat16 [1024, 8192], P('img', 'tp'), may hold values from -0.1875 to 0.1875
- up_bias: float32 [8192], P('tp'), may hold values from -3 to 3
- down_weight: bfloat16 [8192, 4096], P('tp', 'img'), may hold values from -0.125 to 0.125
- down_bias: float32 [4096], replicated, may hold values from -3 to 3
Outputs:
- projected: bfloat16 [32768, 4096], P(('img', 'tp'))
All inputs are finite; a program needn't handle non-finite values.
Results may differ from a plain program's by a relative error of at most 0.014.
Values may be sent and summed in bfloat16 or wider, within the bound.
A program may use at most 128 MiB of HBM per device.

v0:
```python
import jax
import jax.numpy as jnp
from jax import lax
from jax.sharding import PartitionSpec as P


def laid_out(parts, dim):
    dims = list(parts.shape[1:])
    dims[dim] *= parts.shape[0]
    return jnp.moveaxis(parts, 0, dim).reshape(dims)


def from_everyone(x, axis):
    copies = jnp.broadcast_to(x, (lax.axis_size(axis), *x.shape))
    return lax.all_to_all(copies, axis, split_axis=0, concat_axis=0, tiled=True)


def gather_directly(x, axis, dim):
    return laid_out(from_everyone(x, axis), dim)


def on_device(patch_tokens, norm_gain, norm_bias, up_weight, up_bias, down_weight, down_bias):
    values = lax.all_gather(patch_tokens, "tp", axis=0, tiled=True).astype(jnp.float32)
    center = jnp.mean(values, axis=1, keepdims=True)
    spread = jnp.mean((values - center) ** 2, axis=1, keepdims=True)
    gathered = ((values - center) * lax.rsqrt(spread + 1e-05) * norm_gain + norm_bias).astype(
        jnp.bfloat16
    )
    summed = jnp.dot(
        gathered, gather_directly(up_weight, "img", 0), preferred_element_type=jnp.float32
    )
    hidden = jax.nn.gelu(summed + up_bias).astype(jnp.bfloat16)
    down_full = lax.all_gather(down_weight, "img", axis=1, tiled=True)
    total = lax.psum_scatter(
        jnp.dot(hidden, down_full, preferred_element_type=jnp.float32).astype(jnp.bfloat16),
        "tp",
        scatter_dimension=0,
        tiled=True,
    ).astype(jnp.float32)
    return (total + down_bias).astype(jnp.bfloat16)


def solution(mesh):
    return jax.shard_map(
        on_device,
        mesh=mesh,
        in_specs=(P(("img", "tp"), None), P(), P(), P("img", "tp"), P("tp"), P("tp", "img"), P()),
        out_specs=P(("img", "tp"), None),
        check_vma=False,
    )
```

profile of v0, /device:TPU:1, one launch (start us, length us, event | category | flops | bytes accessed | tf_op | source)
XLA Modules:
  0.0 372.6 jit_solution(12355794440621910350)
XLA Ops:
  6.5 0.0 all-gather.3.cloned.1.call-start
  6.5 0.7 all-gather.3.cloned.1.call-update
  7.3 0.0 all-gather.5.cloned.1.call-start
  7.3 0.7 all-gather.5.cloned.1.call-update
  8.0 1.9 broadcast_in_dim.2
  9.9 7.2 %all-to-all-start = ((bf16[16,64,512]{2,1,0:T(8,128)(2,1)}), bf16[16,64,512]{2,1,0:T(8,128)(2,1)S(1)}, u32[]{:S(2)}, u32[]{:S(2)}) async-start(bf16[16,64,512]{2,1,0:T(8,128)(2,1)} %broadcast_in_dim.2), calls=%async_computation | async-start | bytes 2097152 | tf_op jit(solution)/shard_map/all_to_all | solution.py:15
  17.1 0.0 copy-start.2
  17.1 0.0 copy-start.3
  17.1 0.0 copy-start.4
  17.1 0.0 reduce-scatter.2.cloned.1.call-start
  17.2 72.1 %all-gather.3.cloned.1.call-done = bf16[2048,1024]{1,0:T(8,128)(2,1)} async-done(((bf16[128,1024]{1,0:T(8,128)(2,1)}), bf16[2048,1024]{1,0:T(8,128)(2,1)}) %all-gather.3.cloned.1.call-update) | async-done | bytes 4194320 | tf_op jit(solution)/shard_map/all_gather | solution.py:23
  89.2 3.0 convert_reduce_fusion
  92.2 0.5 copy-done
  92.7 1.4 fusion.2
  94.1 0.0 all-to-all-done
  94.1 47.1 %all-gather.5.cloned.1.call-done = bf16[512,4096]{1,0:T(8,128)(2,1)} async-done(((bf16[512,256]{1,0:T(8,128)(2,1)}), bf16[512,4096]{1,0:T(8,128)(2,1)}) %all-gather.5.cloned.1.call-update) | async-done | bytes 4194320 | tf_op jit(solution)/shard_map/all_gather | solution.py:33
  141.1 0.0 copy-done.2
  141.1 0.0 copy-done.3
  141.1 0.0 copy-done.4
  141.1 18.0 %convolution_convert_fusion = bf16[2048,4096]{1,0:T(8,128)(2,1)} fusion(bf16[512,4096]{1,0:T(8,128)(2,1)} %all-gather.5.cloned.1.call-done, bf16[1024,512]{1,0:T(8,128)(2,1)S(1)} %bitcast.3, bf16[2048,1024]{1,0:T(8,128)(2,1)} %all-gather.3.cloned.1.call-done, f32[1024]{0:T(1024)S(1)} %copy-done.2, f32[1024]{0:T(1024)S(1)} %copy-done.3, ...), kind=kOutput, calls=%fused_computation | convolution fusion | flops 10768875520 | bytes 26241024 | tf_op jit(solution)/shard_map/dot_general | solution.py:35
  159.1 0.0 reduce-scatter.2.cloned.1.call-update
  159.1 204.5 %reduce-scatter.2.cloned.1.call-done = bf16[128,4096]{1,0:T(8,128)(2,1)} async-done(((bf16[2048,4096]{1,0:T(8,128)(2,1)}), bf16[128,4096]{1,0:T(8,128)(2,1)}) %reduce-scatter.2.cloned.1.call-update) | async-done | bytes 1048592 | tf_op jit(solution)/shard_map/reduce_scatter | solution.py:34
  363.7 0.0 copy-done.1
  363.7 2.4 add_convert_fusion
  (4 shorter events, 0.0 us)
Async XLA Ops:
  6.5 82.7 %all-gather.3.cloned.1.call-start = ((), (), s32[]{:S(2)}) async-start(), calls=%async_computation.2 | async-start | bytes 4456448 | tf_op jit(solution)/shard_map/all_gather | solution.py:23
  7.3 133.9 %all-gather.5.cloned.1.call-start = ((), (), s32[]{:S(2)}) async-start(), calls=%async_computation.3 | async-start | bytes 4456448 | tf_op jit(solution)/shard_map/all_gather | solution.py:33
  9.9 84.1 %all-to-all-start = ((bf16[16,64,512]{2,1,0:T(8,128)(2,1)}), bf16[16,64,512]{2,1,0:T(8,128)(2,1)S(1)}, u32[]{:S(2)}, u32[]{:S(2)}) async-start(bf16[16,64,512]{2,1,0:T(8,128)(2,1)} %broadcast_in_dim.2), calls=%async_computation | async-start | bytes 2097152 | tf_op jit(solution)/shard_map/all_to_all | solution.py:15
  17.1 124.0 %copy-start.2 = (f32[1024]{0:T(1024)S(1)}, f32[1024]{0:T(1024)}, u32[]{:S(2)}) copy-start(f32[1024]{0:T(1024)} %param.9) | copy-start | bytes 12292
  17.1 124.0 %copy-start.3 = (f32[1024]{0:T(1024)S(1)}, f32[1024]{0:T(1024)}, u32[]{:S(2)}) copy-start(f32[1024]{0:T(1024)} %param.8) | copy-start | bytes 12292
  17.1 124.0 %copy-start.4 = (f32[512]{0:T(512)S(1)}, f32[512]{0:T(512)}, u32[]{:S(2)}) copy-start(f32[512]{0:T(512)} %param.11) | copy-start | bytes 6148
  17.1 346.6 %reduce-scatter.2.cloned.1.call-start = ((), (), s32[]{:S(2)}) async-start(), calls=%async_computation.4 | async-start | bytes 17825792 | tf_op jit(solution)/shard_map/reduce_scatter | solution.py:34
  89.2 3.4 copy-start
  159.1 204.6 %copy-start.1 = (f32[4096]{0:T(1024)S(1)}, f32[4096]{0:T(1024)}, u32[]{:S(2)}) copy-start(f32[4096]{0:T(1024)} %param.13) | copy-start | bytes 49156
Sparse Core Ops, SparseCore 0:
  9.8 79.4 all-gather.2
  91.0 50.1 all-gather.4
  159.3 204.3 reduce-scatter.1
where the time goes:
time: 373 us
  waiting for transfers between devices  325 us (87%)
  matrix products  18 us (5%)
  between operations  13.2 us (4%)
  starting transfers between devices  7.24 us (2%)
  other arithmetic  6.74 us (2%)
    reduce_scatter x1, waiting for transfers between devices, on_device(): lax.psum_scatter(jnp.dot(hidden, down_full, preferred_element_type=jnp.fl...  205 us
    all_gather x1, waiting for transfers between devices, on_device(): lax.all_gather(patch_tokens, 'tp', axis=0, tiled=True).astype(jnp.float32)  72.1 us
    all_gather x1, waiting for transfers between devices, on_device(): down_full = lax.all_gather(down_weight, 'img', axis=1, tiled=True)  47.1 us
    dot_general x1, matrix products, on_device(): jnp.dot(hidden, down_full, preferred_element_type=jnp.float32)  18 us
  transfers between devices with their start and end apart: 4, of which 3 were waited for; matrix products, arithmetic and copies ran while one was open for 2% of the time, Pallas kernels for 0%

commit v1 on v0

v1 whole, which is shorter than its diff:
```python
import jax
import jax.numpy as jnp
from jax import lax
from jax.experimental import pallas as pl
from jax.experimental.pallas import tpu as pltpu
from jax.sharding import PartitionSpec as P

MESH = pl.DeviceIdType.MESH
F32, BF16 = jnp.float32, jnp.bfloat16

WAIT, SEND, SHARE_U, SHARE_D, NORM, HIDDEN, PART, RELAY, FINAL = range(9)
XP, XQ, YP, YQ, ZP, ZQ = range(6)
WU, D0, D1, TOK, SIB_U, SIB_D, FAR, NEAR_P, NEAR_Q = range(9)

STEPS = (
    (SEND, YP, TOK, 0), (SEND, YQ, TOK, 0), (SEND, XP, WU, 0, 0), (SEND, XQ, WU, 0, 0), (SEND, ZP, WU, 0, 0),
    (SEND, ZQ, WU, 0, 0), (SEND, XP, D0, 0, 0), (SEND, XQ, D0, 0, 0), (SEND, ZP, D0, 0, 0), (SEND, ZQ, D0, 0, 0),
    (WAIT, WU, -1, 0), (SEND, XP, WU, -1, 0), (WAIT, WU, 1, 0), (WAIT, WU, 0, -1), (SEND, XQ, WU, 0, -1),
    (SEND, ZP, WU, 0, -1), (SEND, XP, WU, 0, -1), (SEND, ZP, D1, 0, 0), (WAIT, WU, 0, 1), (SEND, ZQ, WU, 0, 1),
    (SEND, XQ, WU, 0, 1), (SEND, ZQ, D1, 0, 0), (SEND, XP, WU, 0, 1), (SEND, XQ, D1, 0, 0), (WAIT, D0, -1, 0),
    (WAIT, D0, 1, 0), (WAIT, D0, 0, -1), (WAIT, D0, 0, 1), (WAIT, WU, 2, 0), (WAIT, WU, 1, -1), (WAIT, TOK, -1),
    (SEND, YP, TOK, -1), (WAIT, TOK, 1), (WAIT, WU, 0, -2), (SEND, XP, WU, 0, -2), (SEND, ZP, WU, 0, -2),
    (SEND, XQ, WU, 0, -2), (SEND, ZP, D0, 0, -1), (WAIT, WU, 0, 2), (SEND, ZQ, WU, 0, 2), (SEND, XP, WU, 0, 2),
    (SEND, ZQ, D0, 0, 1), (SEND, XQ, WU, 0, 2), (SHARE_U, 0), (WAIT, WU, -1, -1), (SEND, XP, WU, -1, -1),
    (WAIT, WU, 1, 1), (WAIT, SIB_U, 0), (WAIT, WU, -1, 1), (SEND, XP, WU, -1, 1), (WAIT, D1, 0, -1),
    (WAIT, D1, 0, 1), (SEND, ZQ, D1, 0, 1), (WAIT, WU, -1, -2), (SEND, XP, WU, -1, -2), (WAIT, D1, 1, 0),
    (WAIT, WU, 0, -3), (SEND, XQ, WU, 0, -3), (SEND, ZP, WU, 0, -3), (SEND, ZP, D1, 0, -1), (SEND, XP, WU, 0, -3),
    (WAIT, WU, 0, 3), (SEND, XQ, WU, 0, 3), (SEND, XQ, D1, 0, -1), (SEND, XP, WU, 0, 3), (WAIT, TOK, 2), (NORM,),
    (WAIT, WU, -1, 2), (SEND, XP, WU, -1, 2), (WAIT, WU, 1, -2), (WAIT, WU, 2, -1), (WAIT, WU, 1, 2),
    (WAIT, D0, 0, -2), (SEND, ZP, D0, 0, -2), (WAIT, D0, 0, 2), (SEND, ZQ, D0, 0, 2), (SHARE_U, -1),
    (WAIT, WU, 2, 1), (WAIT, WU, 1, -3), (WAIT, WU, 0, -4), (SEND, XQ, WU, 0, -4), (SEND, XP, WU, 0, -4),
    (SEND, XQ, D1, 0, 1), (SHARE_U, 1), (WAIT, SIB_U, 1), (WAIT, WU, 2, -2), (WAIT, WU, 1, 3), (WAIT, D1, 0, 2),
    (SEND, ZQ, D1, 0, 2), (SEND, ZQ, D0, -1, 0), (SEND, XQ, D1, 0, 2), (SEND, ZQ, D0, 1, 0), (SHARE_U, -2),
    (WAIT, SIB_U, -1), (WAIT, WU, -1, -3), (SEND, XP, WU, -1, -3), (WAIT, D1, 0, -2), (SEND, ZP, D1, 0, -2),
    (SEND, XQ, D1, 0, -2), (WAIT, SIB_U, 2), (WAIT, WU, -1, 3), (SEND, XP, WU, -1, 3), (WAIT, D1, 1, -1),
    (WAIT, D0, 0, 3), (WAIT, WU, 2, 2), (WAIT, WU, 1, -4), (WAIT, D0, 0, -3), (SEND, ZP, D0, 0, -3), (SHARE_U, 2),
    (SHARE_D, 0, 0, 1), (WAIT, WU, -1, -4), (SEND, XP, WU, -1, -4), (SEND, XP, D0, -1, 0), (SEND, XP, D1, 0, 0),
    (SEND, XP, D1, 0, -1), (SEND, XP, D1, 0, 1), (SEND, XP, D1, 0, 2), (SEND, XP, D1, 0, -2), (WAIT, D1, 0, 3),
    (SEND, XQ, D1, 0, 3), (SEND, XP, D1, 0, 3), (WAIT, SIB_U, -2), (WAIT, WU, 2, -3), (WAIT, D1, 1, 1),
    (WAIT, D1, 0, -3), (SEND, ZP, D1, 0, -3), (SEND, ZP, D0, -1, 0), (SEND, XQ, D1, 0, -3), (SEND, ZP, D0, 1, 0),
    (SEND, XP, D1, 0, -3), (WAIT, SIB_D, 0, 0, 1), (SHARE_U, -3), (SHARE_D, 1, 0, 1), (WAIT, WU, 2, 3),
    (WAIT, D0, -1, 1), (SEND, ZQ, D0, -1, 1), (SHARE_U, 3), (WAIT, SIB_U, 3), (WAIT, WU, 2, -4), (WAIT, D1, 1, 2),
    (WAIT, D0, 0, -4), (WAIT, SIB_D, 1, 0, 1), (SHARE_U, -4), (SHARE_D, 0, 0, 0), (WAIT, SIB_U, -3),
    (WAIT, D0, 1, 1), (SEND, ZQ, D0, 1, 1), (WAIT, SIB_U, -4), (HIDDEN,), (WAIT, D0, 2, 0), (SEND, ZP, D0, 2, 0),
    (SEND, ZQ, D0, 2, 0), (WAIT, D1, 1, -2), (WAIT, D1, 0, -4), (SEND, XQ, D1, 0, -4), (SEND, XP, D1, 0, -4),
    (WAIT, SIB_D, 0, 0, 0), (WAIT, D0, -1, 2), (SEND, ZQ, D0, -1, 2), (WAIT, D1, -1, 0), (SEND, XP, D1, -1, 0),
    (WAIT, D1, 1, 3), (WAIT, D0, -1, -1), (SEND, ZP, D0, -1, -1), (SHARE_D, 1, 0, 0), (PART, 0, 0, 0),
    (WAIT, D0, 1, 2), (SEND, ZQ, D0, 1, 2), (WAIT, D0, 1, -1), (SEND, ZP, D0, 1, -1), (PART, 0, 0, 1),
    (WAIT, D1, -1, -1), (SEND, XP, D1, -1, -1), (WAIT, D1, 1, -3), (WAIT, SIB_D, 1, 0, 0), (SHARE_D, 1, 1, 1),
    (PART, 1, 0, 0), (PART, 1, 0, 1), (WAIT, D1, -1, 1), (SEND, XP, D1, -1, 1), (WAIT, D0, 2, -1), (WAIT, D0, 2, 1),
    (SEND, ZQ, D0, 2, 1), (WAIT, FAR, 0, 0, 0), (WAIT, NEAR_P, 0, 0, 0), (WAIT, D1, 1, -4), (WAIT, SIB_D, 1, -1, 1),
    (SHARE_D, 1, 1, 0), (RELAY, 0, 0, 0), (WAIT, D1, -1, 2), (SEND, XP, D1, -1, 2), (WAIT, FAR, 0, 0, 1),
    (WAIT, NEAR_P, 0, 0, 1), (RELAY, 0, 0, 1), (WAIT, D1, -1, -2), (SEND, XP, D1, -1, -2), (WAIT, SIB_D, 1, -1, 0),
    (WAIT, D0, -1, -2), (SEND, ZP, D0, -1, -2), (SEND, ZP, D0, 2, -1), (WAIT, D0, -1, 3), (WAIT, FAR, 1, 0, 0),
    (WAIT, NEAR_P, 1, 0, 0), (RELAY, 1, 0, 0), (WAIT, D1, -1, 3), (SEND, XP, D1, -1, 3), (WAIT, FAR, 1, 0, 1),
    (WAIT, NEAR_P, 1, 0, 1), (RELAY, 1, 0, 1), (WAIT, NEAR_Q, 0, 0, 0), (FINAL, 0, 0, 0), (WAIT, D1, -1, -3),
    (SEND, XP, D1, -1, -3), (SHARE_D, 1, -1, 1), (PART, 1, -1, 1), (WAIT, D0, 1, -2), (SEND, ZP, D0, 1, -2),
    (WAIT, D0, 1, 3), (WAIT, NEAR_Q, 0, 0, 1), (WAIT, NEAR_Q, 1, 0, 0), (FINAL, 0, 0, 1), (WAIT, D1, -1, -4),
    (SEND, XP, D1, -1, -4), (SHARE_D, 1, -1, 0), (PART, 1, -1, 0), (WAIT, NEAR_Q, 1, 0, 1), (WAIT, SIB_D, 1, 1, 1),
    (WAIT, D1, 2, 0), (PART, 1, 1, 1), (WAIT, D0, -1, -3), (SEND, ZP, D0, -1, -3), (WAIT, D0, 2, 2),
    (SEND, ZQ, D0, 2, 2), (WAIT, SIB_D, 1, 1, 0), (SHARE_D, 0, -1, 1), (PART, 1, 1, 0), (WAIT, D1, 2, -1),
    (WAIT, D0, 2, -2), (WAIT, FAR, 1, -1, 1), (WAIT, NEAR_P, 1, -1, 1), (RELAY, 1, -1, 1), (FINAL, 1, 0, 0),
    (WAIT, D1, 2, 1), (FINAL, 1, 0, 1), (WAIT, D0, 1, -3), (SEND, ZP, D0, 1, -3), (SEND, ZP, D0, 2, -2),
    (SHARE_D, 0, 1, 1), (WAIT, FAR, 1, -1, 0), (WAIT, NEAR_P, 1, -1, 0), (RELAY, 1, -1, 0), (WAIT, SIB_D, 0, 1, 1),
    (PART, 0, 1, 1), (WAIT, D1, 2, 2), (WAIT, FAR, 1, 1, 1), (WAIT, NEAR_P, 1, 1, 1), (RELAY, 1, 1, 1),
    (WAIT, SIB_D, 0, -1, 1), (PART, 0, -1, 1), (WAIT, D1, 2, -2), (WAIT, D0, -1, -4), (WAIT, D0, 2, 3),
    (WAIT, FAR, 1, 1, 0), (WAIT, NEAR_P, 1, 1, 0), (SHARE_D, 0, -1, 0), (RELAY, 1, 1, 0), (WAIT, NEAR_Q, 1, -1, 1),
    (WAIT, D1, 2, 3), (FINAL, 1, -1, 1), (WAIT, D0, 1, -4), (SHARE_D, 0, 1, 0), (WAIT, NEAR_P, 0, 1, 1),
    (WAIT, NEAR_Q, 1, -1, 0), (FINAL, 1, -1, 0), (WAIT, D1, 2, -3), (SHARE_D, 1, 2, 1), (WAIT, D0, 2, -3),
    (SEND, ZP, D0, 2, -3), (SHARE_D, 0, 2, 1), (WAIT, SIB_D, 0, 1, 0), (PART, 0, 1, 0), (WAIT, FAR, 0, 1, 1),
    (WAIT, D1, 2, -4), (WAIT, NEAR_P, 0, -1, 1), (WAIT, SIB_D, 0, -1, 0), (WAIT, NEAR_Q, 1, 1, 1),
    (SHARE_D, 1, 2, 0), (RELAY, 0, 1, 1), (PART, 0, -1, 0), (WAIT, FAR, 0, -1, 1), (WAIT, SIB_D, 1, 2, 1),
    (WAIT, NEAR_Q, 1, 1, 0), (RELAY, 0, -1, 1), (PART, 1, 2, 1), (WAIT, SIB_D, 0, 2, 1), (WAIT, D0, 2, -4),
    (WAIT, SIB_D, 1, 2, 0), (SHARE_D, 0, 2, 0), (PART, 0, 2, 1), (WAIT, FAR, 0, 1, 0), (WAIT, NEAR_P, 0, 1, 0),
    (RELAY, 0, 1, 0), (PART, 1, 2, 0), (WAIT, NEAR_Q, 0, 1, 1), (WAIT, NEAR_P, 0, -1, 0), (WAIT, SIB_D, 0, 2, 0),
    (PART, 0, 2, 0), (WAIT, FAR, 0, -1, 0), (WAIT, NEAR_P, 1, 2, 1), (RELAY, 0, -1, 0), (FINAL, 0, 1, 1),
    (FINAL, 1, 1, 0), (FINAL, 1, 1, 1), (WAIT, NEAR_Q, 0, -1, 1), (FINAL, 0, -1, 1), (WAIT, NEAR_P, 0, 2, 1),
    (WAIT, FAR, 1, 2, 1), (RELAY, 1, 2, 1), (WAIT, NEAR_P, 1, 2, 0), (WAIT, FAR, 0, 2, 1), (RELAY, 0, 2, 1),
    (WAIT, NEAR_P, 0, 2, 0), (WAIT, NEAR_Q, 0, 1, 0), (FINAL, 0, 1, 0), (WAIT, FAR, 1, 2, 0), (RELAY, 1, 2, 0),
    (WAIT, FAR, 0, 2, 0), (RELAY, 0, 2, 0), (WAIT, NEAR_Q, 0, -1, 0), (FINAL, 0, -1, 0), (WAIT, NEAR_Q, 1, 2, 1),
    (FINAL, 1, 2, 1), (WAIT, NEAR_Q, 0, 2, 1), (FINAL, 0, 2, 1), (WAIT, NEAR_Q, 1, 2, 0), (FINAL, 1, 2, 0),
    (WAIT, NEAR_Q, 0, 2, 0), (FINAL, 0, 2, 0),
)

KINDS = (WU, D0, D1)
ITEMS = [(h, dx, rp) for h in (0, 1) for dx in (0, -1, 1, 2) for rp in (0, 1)]
OFFSETS = (0, -1, 1, -2, 2, -3, 3, -4)
AFTER = {XP: -1, XQ: 1, YP: -1, YQ: 1, ZP: -1, ZQ: 1}


def slot(dx):
    return dx % 4


def piece_index(kind, dx, dz):
    return KINDS.index(kind) * 32 + slot(dx) * 8 + dz % 8


def kernel(
    tok, gain, nbias, up, upb, down, dbias, out,
    X, N, U, UB, D, H, A0, A1, S1, S2, S3, RL, FP, FQ,
    loc, wsend, wrecv, xsend, xrecv, bsend, brecv, sibs, sibr, ysend, yrecv,
):
    img, tp = lax.axis_index("img"), lax.axis_index("tp")
    c = lax.rem(img, 2)
    zlo = lax.rem(img // 2, 2)
    x = img // 4
    zhi = lax.rem(tp, 4)
    y = tp // 4
    z = zhi * 2 + zlo
    sign = 1 - 2 * c

    def wrap(v, n):
        return lax.rem(v + 2 * n, n)

    def at(dx=0, dy=0, dz=0, core=None):
        xx, yy, zz = wrap(x + sign * dx, 4), wrap(y + sign * dy, 4), wrap(z + sign * dz, 8)
        cc = c if core is None else core
        return {"img": xx * 4 + lax.rem(zz, 2) * 2 + cc, "tp": yy * 4 + zz // 2}

    sibling = at(core=1 - c)
    link = {
        XP: at(dx=1), XQ: at(dx=-1), YP: at(dy=1), YQ: at(dy=-1), ZP: at(dz=1), ZQ: at(dz=-1),
    }
    far = (at(dz=2), at(dz=-2), at(dz=4))

    copies = [
        pltpu.make_async_copy(tok, X.at[0], loc.at[0]),
        pltpu.make_async_copy(up, U.at[zhi, x, zlo, c], loc.at[1]),
        pltpu.make_async_copy(down.at[:, pl.ds(0, 128)], D.at[0, 0, 0, zhi, :, pl.ds(0, 128)], loc.at[2]),
        pltpu.make_async_copy(down.at[:, pl.ds(128, 128)], D.at[1, 0, 0, zhi, :, pl.ds(0, 128)], loc.at[3]),
        pltpu.make_async_copy(upb, UB.at[zhi], loc.at[4]),
    ]
    for copy in copies:
        copy.start()
    barrier = pltpu.get_barrier_semaphore()
    partners = [sibling, *link.values(), *far]
    for device in partners:
        pl.semaphore_signal(barrier, inc=1, device_id=device, device_id_type=MESH)
    pl.semaphore_wait(barrier, len(partners))
    for copy in copies:
        copy.wait()

    sends = []

    def send(src, dst, ssem, rsem, device):
        copy = pltpu.make_async_remote_copy(
            src_ref=src, dst_ref=dst, send_sem=ssem, recv_sem=rsem, device_id=device, device_id_type=MESH
        )
        copy.start()
        sends.append(copy)

    def arrive(ref, rsem):
        pltpu.make_async_remote_copy(
            src_ref=ref, dst_ref=ref, send_sem=rsem, recv_sem=rsem, device_id=sibling, device_id_type=MESH
        ).wait_recv()

    def where(kind, dx, dz):
        zz = wrap(z + sign * dz, 8)
        if kind == WU:
            return U.at[zz // 2, wrap(x + sign * dx, 4), lax.rem(zz, 2), c]
        return D.at[kind - D0, slot(dx), dz % 2, zz // 2, :, pl.ds(0, 128)]

    def place(kind, dx, dz, dx_there, dz_there):
        if kind == WU:
            return where(kind, dx, dz)
        zz = wrap(z + sign * dz, 8)
        return D.at[kind - D0, slot(dx_there), dz_there % 2, zz // 2, :, pl.ds(0, 128)]

    used = [0, 0]

    def forward(path, kind, dx, dz):
        step = AFTER[path]
        dx_there, dz_there = (dx + step, dz) if path in (XP, XQ) else (dx, dz + step)
        send(
            where(kind, dx, dz),
            place(kind, dx, dz, dx_there, dz_there),
            wsend.at[used[0]],
            wrecv.at[piece_index(kind, dx_there, dz_there)],
            link[path],
        )
        used[0] += 1

    def forward_tokens(path, dy):
        there = slot(dy + AFTER[path])
        send(X.at[slot(dy)], X.at[there], xsend.at[there - 1], xrecv.at[there - 1], link[path])

    def send_y(src, dst, rsem, device):
        send(src, dst, ysend.at[used[1]], rsem, device)
        used[1] += 1

    for i, device in enumerate(far):
        send(UB.at[zhi], UB.at[zhi], bsend.at[i], brecv.at[i], device)

    for step in STEPS:
        op, args = step[0], step[1:]
        if op == SEND:
            if args[1] == TOK:
                forward_tokens(args[0], args[2])
            else:
                forward(*args)
        elif op == WAIT:
            kind = args[0]
            if kind == TOK:
                arrive(X.at[slot(args[1])], xrecv.at[slot(args[1]) - 1])
            elif kind in KINDS:
                arrive(where(*args), wrecv.at[piece_index(*args)])
            elif kind == SIB_U:
                zz = wrap(z + sign * args[1], 8)
                arrive(U.at[zz // 2, :, lax.rem(zz, 2), 1 - c], sibr.at[16 + args[1] % 8])
            elif kind == SIB_D:
                h, dx, rp = args[1:]
                arrive(D.at[h, slot(dx), rp, :, :, pl.ds(128, 128)], sibr.at[ITEMS.index((h, dx, rp))])
            else:
                i = ITEMS.index(args[1:])
                buffer, base = {FAR: (RL, 0), NEAR_P: (FP, 16), NEAR_Q: (FQ, 32)}[kind]
                arrive(buffer.at[i], yrecv.at[base + i])
        elif op == SHARE_U:
            dz = args[0]
            zz = wrap(z + sign * dz, 8)
            block = U.at[zz // 2, :, lax.rem(zz, 2), c]
            send(block, block, sibs.at[16 + dz % 8], sibr.at[16 + (-dz) % 8], sibling)
        elif op == SHARE_D:
            h, dx, rp = args
            i, there = ITEMS.index(args), ITEMS.index((h, -dx if dx in (-1, 1) else dx, rp))
            send(
                D.at[h, slot(dx), rp, :, :, pl.ds(0, 128)],
                D.at[h, slot(-dx), rp, :, :, pl.ds(128, 128)],
                sibs.at[i],
                sibr.at[there],
                sibling,
            )
        elif op == NORM:

            @pl.loop(0, 4)
            def _(r):
                values = X[r].astype(F32)
                center = jnp.mean(values, axis=1, keepdims=True)
                spread = jnp.mean((values - center) ** 2, axis=1, keepdims=True)
                rows = (values - center) * lax.rsqrt(spread + 1e-05) * gain[...] + nbias[...]
                N[pl.ds(pl.multiple_of(r * 128, 128), 128), :] = rows.astype(BF16)

        elif op == HIDDEN:
            for i in range(3):
                zz = wrap(z + sign * (-2, 2, 4)[i], 8)
                arrive(UB.at[zz // 2], brecv.at[i])

            @pl.loop(0, 4)
            def _(g):
                summed = jnp.dot(N[...], U[g].reshape(1024, 512), preferred_element_type=F32)
                hidden = jax.nn.gelu(summed + UB[g], approximate=True)
                H[:, pl.ds(pl.multiple_of(g * 512, 512), 512)] = hidden.astype(BF16)

        elif op == PART:
            h, dx, rp = args
            i = ITEMS.index(args)
            part = jnp.dot(H[...], D[h, slot(dx), rp].reshape(2048, 256), preferred_element_type=F32)
            S2[i] = part[256:384].astype(BF16)
            send_y(S2.at[i], RL.at[i], yrecv.at[i], link[YP])
            S3[i] = part[384:512].astype(BF16)
            send_y(S3.at[i], FP.at[i], yrecv.at[16 + i], link[YQ])
            A0[i] = part[0:128]
            A1[i] = part[128:256]
        elif op == RELAY:
            i = ITEMS.index(args)
            S1[i] = (A1[i] + RL[i].astype(F32)).astype(BF16)
            send_y(S1.at[i], FQ.at[i], yrecv.at[32 + i], link[YP])
        elif op == FINAL:
            h, dx, rp = args
            i = ITEMS.index(args)
            block = wrap(x + sign * dx, 4) * 4 + lax.rem(zlo + rp, 2) * 2
            total = A0[i] + FP[i].astype(F32) + FQ[i].astype(F32)
            for half, core in ((0, c), (1, 1 - c)):
                cols = pl.ds(pl.multiple_of((block + core) * 256 + h * 128, 128), 128)
                out[:, cols] = (total[:, half * 128 : half * 128 + 128] + dbias[:, cols]).astype(BF16)

    for copy in sends:
        copy.wait_send()


def on_device(patch_tokens, norm_gain, norm_bias, up_weight, up_bias, down_weight, down_bias):
    hbm = pl.BlockSpec(memory_space=pl.ANY)
    vmem = pl.BlockSpec(memory_space=pltpu.VMEM)
    dma = pltpu.SemaphoreType.DMA
    return pl.pallas_call(
        kernel,
        out_shape=jax.ShapeDtypeStruct((128, 4096), BF16),
        in_specs=[hbm, vmem, vmem, hbm, hbm, hbm, vmem],
        out_specs=vmem,
        scratch_shapes=[
            pltpu.VMEM((4, 128, 1024), BF16),
            pltpu.VMEM((512, 1024), BF16),
            pltpu.VMEM((4, 4, 2, 2, 64, 512), BF16),
            pltpu.VMEM((4, 1, 512), F32),
            pltpu.VMEM((2, 4, 2, 4, 512, 256), BF16),
            pltpu.VMEM((512, 2048), BF16),
            pltpu.VMEM((16, 128, 256), F32),
            pltpu.VMEM((16, 128, 256), F32),
            *[pltpu.VMEM((16, 128, 256), BF16)] * 6,
            dma((5,)),
            dma((93,)),
            dma((96,)),
            dma((3,)),
            dma((3,)),
            dma((3,)),
            dma((3,)),
            dma((24,)),
            dma((24,)),
            dma((48,)),
            dma((48,)),
        ],
        compiler_params=pltpu.CompilerParams(
            collective_id=0, has_side_effects=True, vmem_limit_bytes=62 * 1024 * 1024
        ),
    )(
        patch_tokens,
        norm_gain.reshape(1, -1),
        norm_bias.reshape(1, -1),
        up_weight,
        up_bias.reshape(1, -1),
        down_weight,
        down_bias.reshape(1, -1),
    )


def solution(mesh):
    return jax.shard_map(
        on_device,
        mesh=mesh,
        in_specs=(P(("img", "tp"), None), P(), P(), P("img", "tp"), P("tp"), P("tp", "img"), P()),
        out_specs=P(("img", "tp"), None),
        check_vma=False,
    )
```

time: 373 us -> 91.3 us (0.24)
  waiting for transfers between devices: 325 us -> 0 us
  Pallas kernels: 0 us -> 88.8 us
  matrix products: 18 us -> 0 us
  between operations: 13.2 us -> 0.01 us
  starting transfers between devices: 7.24 us -> 0 us
  other arithmetic: 6.74 us -> 0 us
    reduce_scatter x1 -> x0, waiting for transfers between devices: 205 us -> none  [on_device(): lax.psum_scatter(jnp.dot(hidden, down_full, preferred_element_type=jnp.fl...]
    all_gather x2 -> x0, waiting for transfers between devices: 119 us -> none  [the longest x1 72.1 us: on_device(): lax.all_gather(patch_tokens, 'tp', axis=0, tiled=True).astype(jnp.float32)]
    pallas_call x0 -> x1, Pallas kernels: none -> 88.8 us  [on_device(): pl.pallas_call(kernel, out_shape=jax.ShapeDtypeStruct((128, 4096), BF16),...]
    dot_general x1 -> x0, matrix products: 18 us -> none  [on_device(): jnp.dot(hidden, down_full, preferred_element_type=jnp.float32)]
    all_to_all x1 -> x0, starting transfers between devices: 7.16 us -> none  [from_everyone(): return lax.all_to_all(copies, axis, split_axis=0, concat_axis=0, tiled=True)]
    reduce_sum x2 -> x0, other arithmetic: 4.33 us -> none  [the longest x1 2.95 us: on_device(): center = jnp.mean(values, axis=1, keepdims=True)]
  transfers between devices with their start and end apart: 4 -> 0, of which waited for: 3 -> 0; matrix products, arithmetic and copies ran while one was open for 2% -> 0% of each run, Pallas kernels for 0% -> 0%
where the time goes in v1:
time: 91.3 us; the launch traced here: 91 us
  Pallas kernels  88.8 us (97%)
  local copies, waits for them, and re-layouts  2.29 us (3%)
    pallas_call x1, Pallas kernels, on_device(): pl.pallas_call(kernel, out_shape=jax.ShapeDtypeStruct((128, 4096), BF16),...  88.8 us
    unnamed x1, local copies, waits for them, and re-layouts  2.29 us

profile of v1, /device:TPU:1, one launch (start us, length us, event | category | flops | bytes accessed | tf_op | source)
XLA Modules:
  0.0 91.0 jit_solution(3939444447409391146)
XLA Ops:
  0.0 88.8 %shard_map.73 = bf16[128,4096]{1,0:T(8,128)(2,1)} custom-call(bf16[128,1024]{1,0:T(8,128)(2,1)} %tok.1, f32[1,1024]{1,0:T(1,128)} %bitcast.5, f32[1,1024]{1,0:T(1,128)} %bitcast.6, bf16[64,512]{1,0:T(8,128)(2,1)} %up.1, f32[1,512]{1,0:T(1,128)} %bitcast.7, bf16[512,256]{1,0:T(8,128)(2,1)} %down.1, f32[1,4096]{1,0:T(1,128)} %bitcast.4), custom_call_target="tpu_custom_call" | custom-call | tf_op jit(solution)/shard_map/pallas_call | solution.py:285
  88.8 2.3 %copy.9 = bf16[128,4096]{1,0:T(8,128)(2,1)} copy(bf16[128,4096]{1,0:T(8,128)(2,1)} %shard_map.73) | data formatting | bytes 2097152

commit v2 on v1

v2 whole, which is shorter than its diff:
```python
import jax
import jax.numpy as jnp
from jax import lax
from jax.experimental import pallas as pl
from jax.experimental.pallas import tpu as pltpu
from jax.sharding import PartitionSpec as P

MESH = pl.DeviceIdType.MESH
F32, BF16 = jnp.float32, jnp.bfloat16

WAIT, SEND, SHARE_U, SHARE_D, NORM, HIDDEN, PART, DIRECT, RELAY, FINAL, LAST = range(11)
XP, XQ, YP, YQ, ZP, ZQ = range(6)
TOK, SIB_U, SIB_D, FAR = range(-4, 0)

WU, D0, D1 = range(3)
PIECES = ((None, 0, 64), (0, 0, 512), (1, 0, 512))
BIASED = WU
FROM_X = (D0,)

STEPS = (
    (SEND, XP, WU, 0, 0), (SEND, XQ, WU, 0, 0), (SEND, YP, TOK, 0), (SEND, YQ, TOK, 0), (SEND, ZP, WU, 0, 0),
    (SEND, ZQ, WU, 0, 0), (SEND, XP, D0, 0, 0), (SEND, XQ, D0, 0, 0), (SEND, ZP, D1, 0, 0), (SEND, ZQ, D1, 0, 0),
    (WAIT, WU, -1, 0), (WAIT, WU, 0, -1), (SEND, XP, WU, 0, -1), (SEND, XQ, WU, 0, -1), (SEND, ZP, WU, 0, -1),
    (SEND, ZP, D0, 0, 0), (WAIT, WU, 0, 1), (SEND, ZQ, WU, 0, 1), (SEND, XP, WU, 0, 1), (SEND, XQ, WU, 0, 1),
    (SEND, ZQ, D0, 0, 0), (SEND, XP, WU, -1, 0), (SEND, XQ, D1, 0, 0), (WAIT, D0, -1, 0), (WAIT, D0, 1, 0),
    (WAIT, D1, 0, -1), (SEND, ZP, D1, 0, -1), (WAIT, D1, 0, 1), (SEND, ZQ, D1, 0, 1), (WAIT, WU, -1, -1),
    (WAIT, TOK, -1), (SEND, YP, TOK, -1), (WAIT, TOK, 1), (WAIT, WU, 0, -2), (SEND, XP, WU, 0, -2),
    (SEND, XQ, WU, 0, -2), (SEND, ZP, WU, 0, -2), (WAIT, WU, 0, 2), (SEND, XP, WU, 0, 2), (SEND, XP, WU, -1, -1),
    (SEND, XQ, WU, 0, 2), (SEND, ZQ, WU, 0, 2), (SEND, XQ, D1, 0, -1), (WAIT, WU, -1, 1), (WAIT, D0, 0, -1),
    (SEND, ZP, D0, 0, -1), (WAIT, D0, 0, 1), (SEND, ZQ, D0, 0, 1), (SHARE_U, 0), (WAIT, WU, -1, -2),
    (SEND, XP, WU, -1, -2), (SEND, XP, WU, -1, 1), (WAIT, SIB_U, 0), (WAIT, TOK, 2), (NORM,), (WAIT, WU, -1, 2),
    (WAIT, D1, 0, -2), (SEND, ZP, D1, 0, -2), (WAIT, D1, 0, 2), (SEND, ZQ, D1, 0, 2), (WAIT, WU, 0, -3),
    (SEND, XP, WU, 0, -3), (SEND, XQ, WU, 0, -3), (SEND, ZP, WU, 0, -3), (WAIT, WU, 0, 3), (SEND, XP, WU, 0, 3),
    (SEND, XQ, WU, 0, 3), (SEND, XP, WU, -1, 2), (SEND, XQ, D1, 0, -2), (SEND, XQ, D1, 0, 2), (SHARE_U, -1),
    (SHARE_U, -2), (WAIT, SIB_U, 1), (WAIT, D0, 0, -2), (SEND, ZP, D0, 0, -2), (WAIT, D0, 0, 2),
    (SEND, ZQ, D0, 0, 2), (SEND, ZQ, D0, -1, 0), (SEND, ZQ, D0, 1, 0), (SHARE_U, 1), (WAIT, SIB_U, 2),
    (WAIT, WU, -1, -3), (SEND, XP, WU, -1, -3), (WAIT, SIB_U, -1), (HIDDEN, 0), (WAIT, WU, -1, 3),
    (SEND, XP, WU, -1, 3), (WAIT, D1, 0, -3), (SEND, ZP, D1, 0, -3), (WAIT, D1, 0, 3), (SHARE_D, 1, 0, 1),
    (WAIT, WU, 0, -4), (SEND, XP, WU, 0, -4), (SEND, XP, D0, -1, 0), (SEND, XQ, WU, 0, -4), (SEND, XQ, D1, 0, 1),
    (SHARE_U, 2), (WAIT, SIB_D, 1, 0, 1), (WAIT, D0, 0, 3), (SHARE_U, -3), (WAIT, SIB_U, -2), (HIDDEN, 1),
    (WAIT, D0, 0, -3), (SEND, ZP, D0, 0, -3), (SEND, ZP, D0, -1, 0), (SHARE_U, 3), (SHARE_D, 0, 0, 1),
    (WAIT, SIB_U, 3), (WAIT, WU, -1, -4), (SEND, XP, WU, -1, -4), (SEND, XP, D1, 0, 0), (SEND, XP, D1, 0, -2),
    (SEND, XP, D1, 0, 2), (WAIT, D0, -1, 1), (SEND, ZQ, D0, -1, 1), (WAIT, SIB_U, -3), (HIDDEN, 2),
    (WAIT, D1, 0, -4), (SEND, XQ, D1, 0, -4), (SEND, XQ, D1, 0, -3), (SEND, XQ, D1, 0, 3), (SEND, XP, D1, 0, -4),
    (SEND, XP, D1, 0, -1), (SEND, XP, D1, 0, 1), (SEND, XP, D1, 0, -3), (SEND, XP, D1, 0, 3), (WAIT, SIB_D, 0, 0, 1),
    (SHARE_D, 1, 0, 0), (WAIT, D0, 2, 0), (SEND, ZQ, D0, 2, 0), (SEND, ZP, D0, 2, 0), (WAIT, D0, 1, 1),
    (SEND, ZQ, D0, 1, 1), (WAIT, D0, 0, -4), (WAIT, SIB_D, 1, 0, 0), (SHARE_U, -4), (SHARE_D, 0, 0, 0),
    (WAIT, D0, -1, 2), (SEND, ZQ, D0, -1, 2), (WAIT, SIB_U, -4), (HIDDEN, 3), (WAIT, D1, -1, 0),
    (SEND, XP, D1, -1, 0), (WAIT, D0, -1, -1), (SEND, ZP, D0, -1, -1), (WAIT, SIB_D, 0, 0, 0), (SHARE_D, 1, 1, 0),
    (PART, 0, 0, 1), (PART, 1, 0, 0), (WAIT, D0, 2, 1), (SEND, ZQ, D0, 2, 1), (PART, 1, 0, 1), (WAIT, D1, -1, -2),
    (SEND, XP, D1, -1, -2), (WAIT, D0, 2, -1), (SEND, ZP, D0, 2, -1), (WAIT, SIB_D, 1, -1, 0), (PART, 0, 0, 0),
    (WAIT, D0, 1, 2), (SEND, ZQ, D0, 1, 2), (WAIT, FAR, 0, 0, 1), (RELAY, 0, 0, 1), (WAIT, D1, -1, 2),
    (SEND, XP, D1, -1, 2), (WAIT, D0, -1, -2), (SEND, ZP, D0, -1, -2), (SHARE_D, 1, 1, 1), (WAIT, FAR, 1, 0, 0),
    (RELAY, 1, 0, 0), (WAIT, D1, -1, -4), (SEND, XP, D1, -1, -4), (WAIT, D0, -1, 3), (SHARE_D, 1, -1, 0),
    (PART, 1, -1, 0), (WAIT, FAR, 1, 0, 1), (RELAY, 1, 0, 1), (WAIT, SIB_D, 1, -1, 1), (WAIT, D1, -1, -1),
    (SEND, XP, D1, -1, -1), (WAIT, D0, 2, -2), (SEND, ZP, D0, 2, -2), (WAIT, FAR, 0, 0, 0), (RELAY, 0, 0, 0),
    (WAIT, SIB_D, 1, 1, 0), (PART, 1, 1, 0), (WAIT, D1, -1, 1), (SEND, XP, D1, -1, 1), (WAIT, D0, 2, 2),
    (SEND, ZQ, D0, 2, 2), (FINAL, 0, 0, 1), (FINAL, 1, 0, 0), (WAIT, D1, -1, -3), (SEND, XP, D1, -1, -3),
    (WAIT, D0, -1, -3), (SEND, ZP, D0, -1, -3), (SEND, ZP, D0, 1, 0), (SHARE_D, 0, -1, 1), (WAIT, FAR, 1, -1, 0),
    (RELAY, 1, -1, 0), (WAIT, D1, -1, 3), (SEND, XP, D1, -1, 3), (WAIT, D0, 1, 3), (SHARE_D, 1, -1, 1),
    (PART, 1, -1, 1), (FINAL, 1, 0, 1), (WAIT, SIB_D, 0, 1, 1), (WAIT, D0, 2, -3), (SEND, ZP, D0, 2, -3),
    (FINAL, 0, 0, 0), (WAIT, FAR, 1, 1, 0), (RELAY, 1, 1, 0), (WAIT, SIB_D, 1, 1, 1), (PART, 1, 1, 1),
    (WAIT, D0, 2, 3), (SHARE_D, 0, 2, 1), (FINAL, 1, -1, 0), (WAIT, D0, -1, -4), (SHARE_D, 0, -1, 0),
    (WAIT, FAR, 1, -1, 1), (RELAY, 1, -1, 1), (WAIT, D0, 1, -1), (SEND, ZP, D0, 1, -1), (SHARE_D, 1, 2, 0),
    (FINAL, 1, 1, 0), (WAIT, SIB_D, 0, 2, 1), (PART, 0, 2, 1), (WAIT, D0, 2, -4), (SHARE_D, 0, 2, 0),
    (WAIT, SIB_D, 0, 1, 0), (WAIT, FAR, 1, 1, 1), (RELAY, 1, 1, 1), (WAIT, SIB_D, 1, 2, 0), (PART, 1, 2, 0),
    (WAIT, D0, 1, -2), (SEND, ZP, D0, 1, -2), (FINAL, 1, -1, 1), (WAIT, SIB_D, 0, 2, 0), (PART, 0, 2, 0),
    (WAIT, FAR, 0, 2, 1), (RELAY, 0, 2, 1), (FINAL, 1, 1, 1), (SHARE_D, 1, 2, 1), (WAIT, FAR, 1, 2, 0),
    (WAIT, D0, 1, -3), (SEND, ZP, D0, 1, -3), (SHARE_D, 0, 1, 1), (RELAY, 1, 2, 0), (PART, 0, 1, 1),
    (WAIT, SIB_D, 1, 2, 1), (PART, 1, 2, 1), (WAIT, FAR, 0, 2, 0), (RELAY, 0, 2, 0), (FINAL, 0, 2, 1),
    (WAIT, SIB_D, 0, -1, 1), (PART, 0, -1, 1), (FINAL, 1, 2, 0), (WAIT, D0, 1, -4), (SHARE_D, 0, 1, 0),
    (PART, 0, 1, 0), (WAIT, FAR, 0, 1, 1), (RELAY, 0, 1, 1), (WAIT, FAR, 1, 2, 1), (WAIT, SIB_D, 0, -1, 0),
    (RELAY, 1, 2, 1), (DIRECT, 0, -1, 0), (FINAL, 0, 2, 0), (WAIT, FAR, 0, -1, 1), (RELAY, 0, -1, 1),
    (WAIT, FAR, 0, 1, 0), (RELAY, 0, 1, 0), (FINAL, 0, 1, 1), (FINAL, 1, 2, 1), (LAST, 0, -1, 0), (FINAL, 0, -1, 1),
    (FINAL, 0, 1, 0),
)

ITEMS = [(h, dx, rp) for h in (0, 1) for dx in (0, -1, 1, 2) for rp in (0, 1)]
OFFSETS = (0, -1, 1, -2, 2, -3, 3, -4)
AFTER = {XP: -1, XQ: 1, YP: -1, YQ: 1, ZP: -1, ZQ: 1}


def slot(dx):
    return dx % 4


def piece_index(kind, dx, dz):
    if kind in FROM_X or slot(dx) in (0, 3):
        return kind * 32 + slot(dx) * 8 + dz % 8
    if PIECES[kind][0] is None:
        return kind * 32 + 8 + dz % 8
    return kind * 32 + slot(dx) * 8 + dz % 2


def piece_semaphore(kind, dx, dz):
    return ARRIVALS.index(piece_index(kind, dx, dz))


ARRIVALS = sorted({piece_index(k, dx, dz) for k in range(len(PIECES)) for dx in (0, -1, 1, 2) for dz in OFFSETS if dx or dz})


def kernel(
    tok, gain, nbias, up, upb, down, dbias, out,
    X, N, U, UB, D, H, O, A0, A1, S1, S2, S3, RL, FP, FQ,
    loc, wsend, wrecv, xsend, xrecv, bsend, brecv, sibs, sibr, ysend, yrecv, stored,
):
    img, tp = lax.axis_index("img"), lax.axis_index("tp")
    c = lax.rem(img, 2)
    zlo = lax.rem(img // 2, 2)
    x = img // 4
    zhi = lax.rem(tp, 4)
    y = tp // 4
    z = zhi * 2 + zlo
    sign = 1 - 2 * c

    def wrap(v, n):
        return lax.rem(v + 2 * n, n)

    def at(dx=0, dy=0, dz=0, core=None):
        xx, yy, zz = wrap(x + sign * dx, 4), wrap(y + sign * dy, 4), wrap(z + sign * dz, 8)
        cc = c if core is None else core
        return {"img": xx * 4 + lax.rem(zz, 2) * 2 + cc, "tp": yy * 4 + zz // 2}

    sibling = at(core=1 - c)
    opposite = at(dy=2)
    link = {
        XP: at(dx=1), XQ: at(dx=-1), YP: at(dy=1), YQ: at(dy=-1), ZP: at(dz=1), ZQ: at(dz=-1),
    }

    copies = [
        pltpu.make_async_copy(tok, X.at[0], loc.at[0]),
        pltpu.make_async_copy(up, U.at[zhi, x, zlo, c], loc.at[1]),
        pltpu.make_async_copy(down.at[:, pl.ds(0, 128)], D.at[0, 0, 0, zhi, :, pl.ds(0, 128)], loc.at[2]),
        pltpu.make_async_copy(down.at[:, pl.ds(128, 128)], D.at[1, 0, 0, zhi, :, pl.ds(0, 128)], loc.at[3]),
        pltpu.make_async_copy(upb, UB.at[z], loc.at[4]),
    ]
    for copy in copies:
        copy.start()
    barrier = pltpu.get_barrier_semaphore()
    partners = [sibling, *link.values(), opposite]
    for device in partners:
        pl.semaphore_signal(barrier, inc=1, device_id=device, device_id_type=MESH)
    pl.semaphore_wait(barrier, len(partners))
    for copy in copies:
        copy.wait()

    def send(src, dst, ssem, rsem, device):
        pltpu.make_async_remote_copy(
            src_ref=src, dst_ref=dst, send_sem=ssem, recv_sem=rsem, device_id=device, device_id_type=MESH
        ).start()

    def arrive(ref, rsem):
        pltpu.make_async_remote_copy(
            src_ref=ref, dst_ref=ref, send_sem=rsem, recv_sem=rsem, device_id=sibling, device_id_type=MESH
        ).wait_recv()

    def where(kind, dx, dz, dx_there=None, dz_there=None):
        half, row, rows = PIECES[kind]
        zz = wrap(z + sign * dz, 8)
        if half is None:
            return U.at[zz // 2, wrap(x + sign * dx, 4), lax.rem(zz, 2), c, pl.ds(row, rows)]
        dx_there = dx if dx_there is None else dx_there
        dz_there = dz if dz_there is None else dz_there
        return D.at[half, slot(dx_there), dz_there % 2, zz // 2, pl.ds(row, rows), pl.ds(0, 128)]

    def some(kind, power):
        half, _, rows = PIECES[kind]
        if half is None:
            whole = U.at[:, :, :, :, pl.ds(0, rows)]
            return (whole.at[0, 0, 0, 0], whole.at[0, 0, 0], whole.at[0, 0], whole.at[0, 0:2], whole.at[0])[power]
        whole = D.at[:, :, :, :, pl.ds(0, rows), pl.ds(0, 128)]
        return (whole.at[0, 0, 0, 0], whole.at[0, 0, 0, 0:2], whole.at[0, 0, 0], whole.at[0, 0], whole.at[0, 0:2])[power]

    sent = [0] * len(PIECES)
    used = [0]

    def forward(path, kind, dx, dz):
        step = AFTER[path]
        dx_there, dz_there = (dx + step, dz) if path in (XP, XQ) else (dx, dz + step)
        send(
            where(kind, dx, dz),
            where(kind, dx, dz, dx_there, dz_there),
            wsend.at[kind * 5 + (sent[kind] + 1).bit_length() - 1],
            wrecv.at[piece_semaphore(kind, dx_there, dz_there)],
            link[path],
        )
        sent[kind] += 1
        if kind == BIASED and path in (ZP, ZQ):
            bias = UB.at[wrap(z + sign * dz, 8)]
            send(bias, bias, bsend.at[0], brecv.at[dz_there % 8], link[path])

    def forward_tokens(path, dy):
        there = slot(dy + AFTER[path])
        send(X.at[slot(dy)], X.at[there], xsend.at[0], xrecv.at[there - 1], link[path])

    def send_y(src, dst, rsem, device):
        send(src, dst, ysend.at[used[0] // 16], rsem, device)
        used[0] += 1

    for step in STEPS:
        op, args = step[0], step[1:]
        if op == SEND:
            if args[1] == TOK:
                forward_tokens(args[0], args[2])
            else:
                forward(*args)
        elif op == WAIT:
            kind = args[0]
            if kind == TOK:
                arrive(X.at[slot(args[1])], xrecv.at[slot(args[1]) - 1])
            elif kind >= 0:
                arrive(where(*args), wrecv.at[piece_semaphore(*args)])
                if kind == BIASED and args[1] == 0:
                    arrive(UB.at[wrap(z + sign * args[2], 8)], brecv.at[args[2] % 8])
            elif kind == SIB_U:
                zz = wrap(z + sign * args[1], 8)
                arrive(U.at[zz // 2, :, lax.rem(zz, 2), 1 - c], sibr.at[16 + args[1] % 8])
            elif kind == SIB_D:
                h, dx, rp = args[1:]
                arrive(D.at[h, slot(dx), rp, :, :, pl.ds(128, 128)], sibr.at[ITEMS.index((h, dx, rp))])
            else:
                i = ITEMS.index(args[1:])
                arrive(RL.at[i], yrecv.at[i])
        elif op == SHARE_U:
            dz = args[0]
            zz = wrap(z + sign * dz, 8)
            block = U.at[zz // 2, :, lax.rem(zz, 2), c]
            for kind, (half, _, _) in enumerate(PIECES):
                if half is None and kind not in FROM_X:
                    arrive(some(kind, 1), wrecv.at[piece_semaphore(kind, 1, dz)])
            send(block, block, sibs.at[1], sibr.at[16 + (-dz) % 8], sibling)
        elif op == SHARE_D:
            h, dx, rp = args
            there = ITEMS.index((h, -dx if dx in (-1, 1) else dx, rp))
            for kind, (half, _, _) in enumerate(PIECES):
                if half == h and kind not in FROM_X and dx in (1, 2):
                    arrive(some(kind, 2), wrecv.at[piece_semaphore(kind, dx, rp)])
            send(
                D.at[h, slot(dx), rp, :, :, pl.ds(0, 128)],
                D.at[h, slot(-dx), rp, :, :, pl.ds(128, 128)],
                sibs.at[0],
                sibr.at[there],
                sibling,
            )
        elif op == NORM:

            @pl.loop(0, 4)
            def _(r):
                values = X[r].astype(F32)
                center = jnp.mean(values, axis=1, keepdims=True)
                spread = jnp.mean((values - center) ** 2, axis=1, keepdims=True)
                rows = (values - center) * lax.rsqrt(spread + 1e-05) * gain[...] + nbias[...]
                N[pl.ds(pl.multiple_of(r * 128, 128), 128), :] = rows.astype(BF16)

        elif op == HIDDEN:
            side = 1 - 2 * zlo
            zz = wrap(z + (0, -2 * side, 2 * side, 4)[args[0]], 8)
            g = zz // 2
            summed = jnp.dot(N[...], U[g].reshape(1024, 512), preferred_element_type=F32)
            hidden = jax.nn.gelu(summed + UB[zz], approximate=True)
            H[:, pl.ds(pl.multiple_of(g * 512, 512), 512)] = hidden.astype(BF16)

        elif op in (PART, DIRECT):
            h, dx, rp = args
            i = ITEMS.index(args)
            columns = D[h, slot(dx), rp].reshape(2048, 256)
            here, there = (jnp.dot(H[m : m + 256], columns, preferred_element_type=F32) for m in (0, 256))
            A0[i] = here[0:128]
            S2[i] = there[0:128].astype(BF16)
            S3[i] = there[128:256].astype(BF16)
            if op == PART:
                A1[i] = here[128:256]
                send_y(S2.at[i], RL.at[i], yrecv.at[i], link[YP])
                send_y(S3.at[i], FP.at[i], yrecv.at[16 + i], link[YQ])
            else:
                S1[i] = here[128:256].astype(BF16)
                send_y(S2.at[i], RL.at[i], yrecv.at[16 + i], opposite)
                send_y(S3.at[i], FP.at[i], yrecv.at[16 + i], link[YQ])
                send_y(S1.at[i], FQ.at[i], yrecv.at[16 + i], link[YP])
        elif op == RELAY:
            i = ITEMS.index(args)
            S1[i] = (A1[i] + RL[i].astype(F32)).astype(BF16)
            send_y(S1.at[i], FQ.at[i], yrecv.at[16 + i], link[YP])
        elif op in (FINAL, LAST):
            h, dx, rp = args
            i = ITEMS.index(args)
            block = wrap(x + sign * dx, 4) * 4 + lax.rem(zlo + rp, 2) * 2
            arrive(FP.at[0 : 2 if op == FINAL else 3], yrecv.at[16 + i])
            total = A0[i] + FP[i].astype(F32) + FQ[i].astype(F32)
            if op == LAST:
                total = total + RL[i].astype(F32)
            for half, core in ((0, c), (1, 1 - c)):
                cols = pl.ds(pl.multiple_of((block + core) * 256 + h * 128, 128), 128)
                O[:, cols] = (total[:, half * 128 : half * 128 + 128] + dbias[:, cols]).astype(BF16)
                pltpu.make_async_copy(O.at[:, cols], out.at[:, cols], stored.at[0]).start()

    def left(ref, ssem):
        pltpu.make_async_remote_copy(
            src_ref=ref, dst_ref=ref, send_sem=ssem, recv_sem=ssem, device_id=sibling, device_id_type=MESH
        ).wait_send()

    left(X.at[0:3], xsend.at[0])
    left(UB.at[0:7], bsend.at[0])
    for kind in range(len(PIECES)):
        for power in range(5):
            left(some(kind, power), wsend.at[kind * 5 + power])
    left(D.at[:, :, :, :, :, pl.ds(0, 128)], sibs.at[0])
    left(U.at[:, :, :, 0], sibs.at[1])
    for i in range(3):
        left(FP, ysend.at[i])
    pltpu.make_async_copy(O, out, stored.at[0]).wait()


def on_device(patch_tokens, norm_gain, norm_bias, up_weight, up_bias, down_weight, down_bias):
    hbm = pl.BlockSpec(memory_space=pltpu.HBM)
    vmem = pl.BlockSpec(memory_space=pltpu.VMEM)
    dma = pltpu.SemaphoreType.DMA
    return pl.pallas_call(
        kernel,
        out_shape=jax.ShapeDtypeStruct((128, 4096), BF16),
        in_specs=[hbm, vmem, vmem, hbm, hbm, hbm, vmem],
        out_specs=hbm,
        scratch_shapes=[
            pltpu.VMEM((4, 128, 1024), BF16),
            pltpu.VMEM((512, 1024), BF16),
            pltpu.VMEM((4, 4, 2, 2, 64, 512), BF16),
            pltpu.VMEM((8, 1, 512), F32),
            pltpu.VMEM((2, 4, 2, 4, 512, 256), BF16),
            pltpu.VMEM((512, 2048), BF16),
            pltpu.VMEM((128, 4096), BF16),
            pltpu.VMEM((16, 128, 256), F32),
            pltpu.VMEM((16, 128, 256), F32),
            *[pltpu.VMEM((16, 128, 256), BF16)] * 6,
            dma((5,)),
            dma((5 * len(PIECES),)),
            dma((len(ARRIVALS),)),
            dma((1,)),
            dma((3,)),
            dma((1,)),
            dma((8,)),
            dma((2,)),
            dma((24,)),
            dma((3,)),
            dma((32,)),
            dma((1,)),
        ],
        compiler_params=pltpu.CompilerParams(
            collective_id=0, has_side_effects=True, vmem_limit_bytes=62 * 1024 * 1024
        ),
    )(
        patch_tokens,
        norm_gain.reshape(1, -1),
        norm_bias.reshape(1, -1),
        up_weight,
        up_bias.reshape(1, -1),
        down_weight,
        down_bias.reshape(1, -1),
    )


def solution(mesh):
    return jax.shard_map(
        on_device,
        mesh=mesh,
        in_specs=(P(("img", "tp"), None), P(), P(), P("img", "tp"), P("tp"), P("tp", "img"), P()),
        out_specs=P(("img", "tp"), None),
        check_vma=False,
    )
```

time: 91.3 us -> 88.6 us (0.970)
  Pallas kernels: 88.8 us -> 86.1 us
    pallas_call x1, Pallas kernels: 88.8 us -> 86.1 us  [on_device(): pl.pallas_call(kernel, out_shape=jax.ShapeDtypeStruct((128, 4096), BF16),...]
where the time goes in v2:
time: 88.6 us; the launch traced here: 88.4 us
  Pallas kernels  86.1 us (97%)
  local copies, waits for them, and re-layouts  2.29 us (3%)
    pallas_call x1, Pallas kernels, on_device(): pl.pallas_call(kernel, out_shape=jax.ShapeDtypeStruct((128, 4096), BF16),...  86.1 us
    unnamed x1, local copies, waits for them, and re-layouts  2.29 us

profile of v2, /device:TPU:1, one launch (start us, length us, event | category | flops | bytes accessed | tf_op | source)
XLA Modules:
  0.0 88.4 jit_solution(17437021218027980567)
XLA Ops:
  0.0 86.1 %shard_map.73 = bf16[128,4096]{1,0:T(8,128)(2,1)} custom-call(bf16[128,1024]{1,0:T(8,128)(2,1)} %tok.1, f32[1,1024]{1,0:T(1,128)} %bitcast.5, f32[1,1024]{1,0:T(1,128)} %bitcast.6, bf16[64,512]{1,0:T(8,128)(2,1)} %up.1, f32[1,512]{1,0:T(1,128)} %bitcast.7, bf16[512,256]{1,0:T(8,128)(2,1)} %down.1, f32[1,4096]{1,0:T(1,128)} %bitcast.4), custom_call_target="tpu_custom_call" | custom-call | tf_op jit(solution)/shard_map/pallas_call | solution.py:318
  86.2 2.3 %copy.9 = bf16[128,4096]{1,0:T(8,128)(2,1)} copy(bf16[128,4096]{1,0:T(8,128)(2,1)} %shard_map.73) | data formatting | bytes 2097152

commit v3 on v2

--- a/solution.py
+++ b/solution.py
@@ -12,67 +12,99 @@
 XP, XQ, YP, YQ, ZP, ZQ = range(6)
 TOK, SIB_U, SIB_D, FAR = range(-4, 0)
 
-WU, D0, D1 = range(3)
-PIECES = ((None, 0, 64), (0, 0, 512), (1, 0, 512))
-BIASED = WU
-FROM_X = (D0,)
+WUA, WUB, D0, D0B, D1, D1B = range(6)
+PIECES = ((None, 0, 32), (None, 32, 32), (0, 0, 384), (0, 384, 128), (1, 0, 256), (1, 256, 256))
+BIASED = WUB
+FROM_X = (WUA, D0,)
 
 STEPS = (
-    (SEND, XP, WU, 0, 0), (SEND, XQ, WU, 0, 0), (SEND, YP, TOK, 0), (SEND, YQ, TOK, 0), (SEND, ZP, WU, 0, 0),
-    (SEND, ZQ, WU, 0, 0), (SEND, XP, D0, 0, 0), (SEND, XQ, D0, 0, 0), (SEND, ZP, D1, 0, 0), (SEND, ZQ, D1, 0, 0),
-    (WAIT, WU, -1, 0), (WAIT, WU, 0, -1), (SEND, XP, WU, 0, -1), (SEND, XQ, WU, 0, -1), (SEND, ZP, WU, 0, -1),
-    (SEND, ZP, D0, 0, 0), (WAIT, WU, 0, 1), (SEND, ZQ, WU, 0, 1), (SEND, XP, WU, 0, 1), (SEND, XQ, WU, 0, 1),
-    (SEND, ZQ, D0, 0, 0), (SEND, XP, WU, -1, 0), (SEND, XQ, D1, 0, 0), (WAIT, D0, -1, 0), (WAIT, D0, 1, 0),
-    (WAIT, D1, 0, -1), (SEND, ZP, D1, 0, -1), (WAIT, D1, 0, 1), (SEND, ZQ, D1, 0, 1), (WAIT, WU, -1, -1),
-    (WAIT, TOK, -1), (SEND, YP, TOK, -1), (WAIT, TOK, 1), (WAIT, WU, 0, -2), (SEND, XP, WU, 0, -2),
-    (SEND, XQ, WU, 0, -2), (SEND, ZP, WU, 0, -2), (WAIT, WU, 0, 2), (SEND, XP, WU, 0, 2), (SEND, XP, WU, -1, -1),
-    (SEND, XQ, WU, 0, 2), (SEND, ZQ, WU, 0, 2), (SEND, XQ, D1, 0, -1), (WAIT, WU, -1, 1), (WAIT, D0, 0, -1),
-    (SEND, ZP, D0, 0, -1), (WAIT, D0, 0, 1), (SEND, ZQ, D0, 0, 1), (SHARE_U, 0), (WAIT, WU, -1, -2),
-    (SEND, XP, WU, -1, -2), (SEND, XP, WU, -1, 1), (WAIT, SIB_U, 0), (WAIT, TOK, 2), (NORM,), (WAIT, WU, -1, 2),
-    (WAIT, D1, 0, -2), (SEND, ZP, D1, 0, -2), (WAIT, D1, 0, 2), (SEND, ZQ, D1, 0, 2), (WAIT, WU, 0, -3),
-    (SEND, XP, WU, 0, -3), (SEND, XQ, WU, 0, -3), (SEND, ZP, WU, 0, -3), (WAIT, WU, 0, 3), (SEND, XP, WU, 0, 3),
-    (SEND, XQ, WU, 0, 3), (SEND, XP, WU, -1, 2), (SEND, XQ, D1, 0, -2), (SEND, XQ, D1, 0, 2), (SHARE_U, -1),
-    (SHARE_U, -2), (WAIT, SIB_U, 1), (WAIT, D0, 0, -2), (SEND, ZP, D0, 0, -2), (WAIT, D0, 0, 2),
-    (SEND, ZQ, D0, 0, 2), (SEND, ZQ, D0, -1, 0), (SEND, ZQ, D0, 1, 0), (SHARE_U, 1), (WAIT, SIB_U, 2),
-    (WAIT, WU, -1, -3), (SEND, XP, WU, -1, -3), (WAIT, SIB_U, -1), (HIDDEN, 0), (WAIT, WU, -1, 3),
-    (SEND, XP, WU, -1, 3), (WAIT, D1, 0, -3), (SEND, ZP, D1, 0, -3), (WAIT, D1, 0, 3), (SHARE_D, 1, 0, 1),
-    (WAIT, WU, 0, -4), (SEND, XP, WU, 0, -4), (SEND, XP, D0, -1, 0), (SEND, XQ, WU, 0, -4), (SEND, XQ, D1, 0, 1),
-    (SHARE_U, 2), (WAIT, SIB_D, 1, 0, 1), (WAIT, D0, 0, 3), (SHARE_U, -3), (WAIT, SIB_U, -2), (HIDDEN, 1),
-    (WAIT, D0, 0, -3), (SEND, ZP, D0, 0, -3), (SEND, ZP, D0, -1, 0), (SHARE_U, 3), (SHARE_D, 0, 0, 1),
-    (WAIT, SIB_U, 3), (WAIT, WU, -1, -4), (SEND, XP, WU, -1, -4), (SEND, XP, D1, 0, 0), (SEND, XP, D1, 0, -2),
-    (SEND, XP, D1, 0, 2), (WAIT, D0, -1, 1), (SEND, ZQ, D0, -1, 1), (WAIT, SIB_U, -3), (HIDDEN, 2),
-    (WAIT, D1, 0, -4), (SEND, XQ, D1, 0, -4), (SEND, XQ, D1, 0, -3), (SEND, XQ, D1, 0, 3), (SEND, XP, D1, 0, -4),
-    (SEND, XP, D1, 0, -1), (SEND, XP, D1, 0, 1), (SEND, XP, D1, 0, -3), (SEND, XP, D1, 0, 3), (WAIT, SIB_D, 0, 0, 1),
-    (SHARE_D, 1, 0, 0), (WAIT, D0, 2, 0), (SEND, ZQ, D0, 2, 0), (SEND, ZP, D0, 2, 0), (WAIT, D0, 1, 1),
-    (SEND, ZQ, D0, 1, 1), (WAIT, D0, 0, -4), (WAIT, SIB_D, 1, 0, 0), (SHARE_U, -4), (SHARE_D, 0, 0, 0),
-    (WAIT, D0, -1, 2), (SEND, ZQ, D0, -1, 2), (WAIT, SIB_U, -4), (HIDDEN, 3), (WAIT, D1, -1, 0),
-    (SEND, XP, D1, -1, 0), (WAIT, D0, -1, -1), (SEND, ZP, D0, -1, -1), (WAIT, SIB_D, 0, 0, 0), (SHARE_D, 1, 1, 0),
-    (PART, 0, 0, 1), (PART, 1, 0, 0), (WAIT, D0, 2, 1), (SEND, ZQ, D0, 2, 1), (PART, 1, 0, 1), (WAIT, D1, -1, -2),
-    (SEND, XP, D1, -1, -2), (WAIT, D0, 2, -1), (SEND, ZP, D0, 2, -1), (WAIT, SIB_D, 1, -1, 0), (PART, 0, 0, 0),
-    (WAIT, D0, 1, 2), (SEND, ZQ, D0, 1, 2), (WAIT, FAR, 0, 0, 1), (RELAY, 0, 0, 1), (WAIT, D1, -1, 2),
-    (SEND, XP, D1, -1, 2), (WAIT, D0, -1, -2), (SEND, ZP, D0, -1, -2), (SHARE_D, 1, 1, 1), (WAIT, FAR, 1, 0, 0),
-    (RELAY, 1, 0, 0), (WAIT, D1, -1, -4), (SEND, XP, D1, -1, -4), (WAIT, D0, -1, 3), (SHARE_D, 1, -1, 0),
-    (PART, 1, -1, 0), (WAIT, FAR, 1, 0, 1), (RELAY, 1, 0, 1), (WAIT, SIB_D, 1, -1, 1), (WAIT, D1, -1, -1),
-    (SEND, XP, D1, -1, -1), (WAIT, D0, 2, -2), (SEND, ZP, D0, 2, -2), (WAIT, FAR, 0, 0, 0), (RELAY, 0, 0, 0),
-    (WAIT, SIB_D, 1, 1, 0), (PART, 1, 1, 0), (WAIT, D1, -1, 1), (SEND, XP, D1, -1, 1), (WAIT, D0, 2, 2),
-    (SEND, ZQ, D0, 2, 2), (FINAL, 0, 0, 1), (FINAL, 1, 0, 0), (WAIT, D1, -1, -3), (SEND, XP, D1, -1, -3),
-    (WAIT, D0, -1, -3), (SEND, ZP, D0, -1, -3), (SEND, ZP, D0, 1, 0), (SHARE_D, 0, -1, 1), (WAIT, FAR, 1, -1, 0),
-    (RELAY, 1, -1, 0), (WAIT, D1, -1, 3), (SEND, XP, D1, -1, 3), (WAIT, D0, 1, 3), (SHARE_D, 1, -1, 1),
-    (PART, 1, -1, 1), (FINAL, 1, 0, 1), (WAIT, SIB_D, 0, 1, 1), (WAIT, D0, 2, -3), (SEND, ZP, D0, 2, -3),
-    (FINAL, 0, 0, 0), (WAIT, FAR, 1, 1, 0), (RELAY, 1, 1, 0), (WAIT, SIB_D, 1, 1, 1), (PART, 1, 1, 1),
-    (WAIT, D0, 2, 3), (SHARE_D, 0, 2, 1), (FINAL, 1, -1, 0), (WAIT, D0, -1, -4), (SHARE_D, 0, -1, 0),
-    (WAIT, FAR, 1, -1, 1), (RELAY, 1, -1, 1), (WAIT, D0, 1, -1), (SEND, ZP, D0, 1, -1), (SHARE_D, 1, 2, 0),
-    (FINAL, 1, 1, 0), (WAIT, SIB_D, 0, 2, 1), (PART, 0, 2, 1), (WAIT, D0, 2, -4), (SHARE_D, 0, 2, 0),
-    (WAIT, SIB_D, 0, 1, 0), (WAIT, FAR, 1, 1, 1), (RELAY, 1, 1, 1), (WAIT, SIB_D, 1, 2, 0), (PART, 1, 2, 0),
-    (WAIT, D0, 1, -2), (SEND, ZP, D0, 1, -2), (FINAL, 1, -1, 1), (WAIT, SIB_D, 0, 2, 0), (PART, 0, 2, 0),
-    (WAIT, FAR, 0, 2, 1), (RELAY, 0, 2, 1), (FINAL, 1, 1, 1), (SHARE_D, 1, 2, 1), (WAIT, FAR, 1, 2, 0),
-    (WAIT, D0, 1, -3), (SEND, ZP, D0, 1, -3), (SHARE_D, 0, 1, 1), (RELAY, 1, 2, 0), (PART, 0, 1, 1),
-    (WAIT, SIB_D, 1, 2, 1), (PART, 1, 2, 1), (WAIT, FAR, 0, 2, 0), (RELAY, 0, 2, 0), (FINAL, 0, 2, 1),
-    (WAIT, SIB_D, 0, -1, 1), (PART, 0, -1, 1), (FINAL, 1, 2, 0), (WAIT, D0, 1, -4), (SHARE_D, 0, 1, 0),
-    (PART, 0, 1, 0), (WAIT, FAR, 0, 1, 1), (RELAY, 0, 1, 1), (WAIT, FAR, 1, 2, 1), (WAIT, SIB_D, 0, -1, 0),
-    (RELAY, 1, 2, 1), (DIRECT, 0, -1, 0), (FINAL, 0, 2, 0), (WAIT, FAR, 0, -1, 1), (RELAY, 0, -1, 1),
-    (WAIT, FAR, 0, 1, 0), (RELAY, 0, 1, 0), (FINAL, 0, 1, 1), (FINAL, 1, 2, 1), (LAST, 0, -1, 0), (FINAL, 0, -1, 1),
-    (FINAL, 0, 1, 0),
+    (SEND, XP, WUA, 0, 0), (SEND, XQ, WUA, 0, 0), (SEND, YP, TOK, 0), (SEND, YQ, TOK, 0), (SEND, ZP, WUA, 0, 0),
+    (SEND, ZQ, WUA, 0, 0), (SEND, XP, D0, 0, 0), (SEND, XQ, WUB, 0, 0), (SEND, ZP, WUB, 0, 0), (SEND, ZQ, WUB, 0, 0),
+    (SEND, XQ, D0, 0, 0), (SEND, ZP, D1, 0, 0), (SEND, ZQ, D1, 0, 0), (SEND, XP, D0B, 0, 0), (SEND, ZP, D1B, 0, 0),
+    (SEND, ZQ, D1B, 0, 0), (SEND, XP, WUB, 0, 0), (SEND, XQ, D0B, 0, 0), (WAIT, WUA, -1, 0), (WAIT, WUA, 1, 0),
+    (SEND, ZP, WUA, 1, 0), (SEND, ZQ, WUA, 1, 0), (SEND, ZP, WUA, -1, 0), (SEND, ZQ, WUA, -1, 0), (WAIT, WUA, 0, -1),
+    (WAIT, WUA, 0, 1), (WAIT, WUB, 0, -1), (SEND, XP, WUB, 0, -1), (SEND, XQ, WUB, 0, -1), (SEND, ZP, WUB, 0, -1),
+    (SEND, ZP, WUA, 0, -1), (WAIT, WUB, 0, 1), (SEND, XP, WUB, 0, 1), (SEND, XQ, WUB, 0, 1), (SEND, XP, WUA, -1, 0),
+    (SEND, ZQ, WUB, 0, 1), (SEND, ZQ, WUA, 0, 1), (WAIT, D0, -1, 0), (WAIT, D1, 0, -1), (SEND, XQ, D1, 0, -1),
+    (SEND, XP, D1, 0, -1), (SEND, ZP, D1, 0, -1), (WAIT, D1, 0, 1), (SEND, XQ, D1, 0, 1), (SEND, ZQ, D1, 0, 1),
+    (WAIT, D0B, -1, 0), (WAIT, D0, 1, 0), (WAIT, WUB, -1, 0), (WAIT, D1B, 0, -1), (SEND, XQ, D1B, 0, -1),
+    (WAIT, D1B, 0, 1), (WAIT, WUB, -1, -1), (SEND, XP, WUB, -1, -1), (WAIT, WUA, 1, -1), (SEND, ZP, WUA, 1, -1),
+    (WAIT, WUA, 1, 1), (SEND, ZQ, WUA, 1, 1), (WAIT, WUB, -1, 1), (SEND, XP, WUB, -1, 1), (SEND, XP, WUB, -1, 0),
+    (WAIT, TOK, -1), (SEND, YP, TOK, -1), (WAIT, TOK, 1), (WAIT, WUA, -1, -1), (WAIT, WUA, -1, 1), (WAIT, WUA, 2, 0),
+    (WAIT, WUB, 0, -2), (SEND, ZP, WUB, 0, -2), (SEND, XP, WUB, 0, -2), (SEND, XQ, WUB, 0, -2), (WAIT, WUB, 0, 2),
+    (SEND, ZQ, WUB, 0, 2), (SEND, XP, WUB, 0, 2), (SEND, XQ, WUB, 0, 2), (SEND, XP, D1, 0, 1), (SEND, XQ, D1B, 0, 1),
+    (WAIT, WUA, 0, -2), (SEND, ZP, WUA, 0, -2), (SEND, ZP, WUA, 2, 0), (SEND, ZP, WUA, -1, -1), (WAIT, WUA, 0, 2),
+    (SEND, ZQ, WUA, 0, 2), (SEND, ZQ, WUA, 2, 0), (SEND, ZQ, WUA, -1, 1), (WAIT, D1, -1, -1), (WAIT, D1, 0, -2),
+    (WAIT, D1, 0, 2), (WAIT, WUA, 1, -2), (SEND, ZP, WUA, 1, -2), (WAIT, WUA, 1, 2), (SEND, ZQ, WUA, 1, 2),
+    (SEND, ZQ, D1B, 0, 1), (SEND, ZQ, D1, 0, 2), (WAIT, WUB, 0, -3), (SEND, XP, WUB, 0, -3), (SEND, XQ, WUB, 0, -3),
+    (SEND, ZP, WUB, 0, -3), (WAIT, WUB, 0, 3), (SEND, XQ, WUB, 0, 3), (SEND, XQ, D1, 0, 0), (SEND, XQ, D1B, 0, 0),
+    (SHARE_U, 0), (WAIT, WUB, -1, -2), (SEND, XP, WUB, -1, -2), (SEND, XP, WUB, 0, 3), (WAIT, WUA, 0, -3),
+    (SEND, ZP, WUA, 0, -3), (SEND, ZP, D1B, 0, -1), (WAIT, WUA, 0, 3), (WAIT, TOK, 2), (NORM,), (WAIT, WUB, -1, 2),
+    (SEND, XP, WUB, -1, 2), (SEND, XP, D1B, 0, -1), (WAIT, WUA, 2, -1), (WAIT, WUA, 2, 1), (WAIT, SIB_U, 0),
+    (WAIT, WUA, -1, -2), (SEND, ZP, WUA, -1, -2), (WAIT, WUA, -1, 2), (SEND, ZQ, WUA, -1, 2), (SEND, ZQ, WUA, 2, 1),
+    (SHARE_U, -1), (SHARE_U, 1), (WAIT, D1, -1, 1), (WAIT, WUA, 1, -3), (SEND, ZP, WUA, 1, -3),
+    (SEND, ZP, WUA, 2, -1), (SEND, ZP, D1, 0, -2), (WAIT, WUA, 1, 3), (WAIT, WUB, -1, -3), (SEND, XP, WUB, -1, -3),
+    (WAIT, WUB, 0, -4), (SEND, XQ, WUB, 0, -4), (SEND, XQ, D1, 0, -2), (WAIT, WUA, 0, -4), (WAIT, D1B, 0, 2),
+    (SEND, ZQ, D1B, 0, 2), (SEND, ZQ, D0, 0, 0), (WAIT, SIB_U, 1), (WAIT, WUB, -1, 3), (SEND, XP, WUB, -1, 3),
+    (SEND, XP, WUB, 0, -4), (SEND, XP, D1B, 0, 1), (WAIT, SIB_U, -1), (HIDDEN, 0), (WAIT, D1B, 0, -2),
+    (WAIT, D1, 0, 3), (SEND, XQ, D1, 0, 3), (SEND, XP, D1, 0, 3), (SEND, XQ, D1, 0, 2), (WAIT, WUA, -1, -3),
+    (SEND, ZP, WUA, -1, -3), (SEND, ZP, D1B, 0, -2), (WAIT, WUA, -1, 3), (WAIT, D1B, -1, -1), (WAIT, WUA, 1, -4),
+    (WAIT, WUA, 2, 2), (SEND, ZQ, WUA, 2, 2), (SEND, ZQ, D0B, 0, 0), (SEND, ZQ, D0, 1, 0), (SHARE_U, 2),
+    (WAIT, WUA, 2, -2), (SEND, ZP, WUA, 2, -2), (SHARE_U, -2), (WAIT, D1B, 0, 3), (SEND, XQ, D1B, 0, 3),
+    (WAIT, SIB_U, -2), (WAIT, WUB, -1, -4), (SEND, XP, WUB, -1, -4), (SEND, XP, D1B, 0, 3), (WAIT, D1, 0, -3),
+    (SEND, ZP, D1, 0, -3), (SEND, XQ, D1, 0, -3), (SEND, ZP, D0, 0, 0), (SEND, XP, D1, 0, -3), (WAIT, SIB_U, 2),
+    (HIDDEN, 1), (WAIT, WUA, -1, -4), (WAIT, D1B, -1, 1), (WAIT, D0, 0, 1), (SEND, ZQ, D0, 0, 1), (WAIT, D1B, 0, -3),
+    (SEND, XP, D1B, 0, -3), (SEND, XP, D1, 0, 0), (SEND, XP, D1B, 0, 0), (WAIT, WUA, 2, 3), (SHARE_D, 1, 0, 1),
+    (SHARE_U, 3), (WAIT, D1, -1, 3), (WAIT, WUA, 2, -3), (SEND, ZP, WUA, 2, -3), (SEND, ZP, D1B, 0, -3),
+    (SEND, ZP, D0B, 0, 0), (WAIT, D0B, 0, 1), (SEND, XQ, D0B, 0, 1), (SEND, XQ, D1B, 0, -3), (SEND, ZQ, D0B, 0, 1),
+    (SEND, XQ, D1B, 0, 2), (SEND, XQ, D1B, 0, -2), (SHARE_U, -3), (WAIT, D1, 0, -4), (WAIT, SIB_D, 1, 0, 1),
+    (WAIT, D1B, -1, 3), (WAIT, D0, 1, 1), (SEND, ZQ, D0, 1, 1), (WAIT, SIB_U, 3), (WAIT, SIB_U, -3), (HIDDEN, 2),
+    (WAIT, D1, -1, -3), (WAIT, D0, 0, -1), (SEND, ZP, D0, 0, -1), (SEND, ZP, D0, 1, 0), (WAIT, WUA, 2, -4),
+    (WAIT, D0, 0, 2), (SEND, ZQ, D0, 0, 2), (SHARE_U, -4), (WAIT, D1B, -1, -3), (WAIT, D0B, 0, 2),
+    (SEND, XQ, D0B, 0, 2), (SEND, XP, D0B, 0, 2), (SEND, XP, D1, 0, -2), (SEND, XQ, D1, 0, -4),
+    (SEND, ZQ, D0B, 0, 2), (SEND, XP, D1, 0, 2), (SEND, XP, D1B, 0, 2), (SEND, XP, D1B, 0, -2),
+    (SEND, XP, D1, 0, -4), (SHARE_D, 1, -1, 1), (SHARE_D, 1, 1, 1), (WAIT, D1B, 0, -4), (SHARE_D, 1, 0, 0),
+    (WAIT, SIB_U, -4), (HIDDEN, 3), (WAIT, D1, -1, 0), (WAIT, D0B, 0, -1), (SEND, XQ, D0B, 0, -1),
+    (SEND, XQ, D1B, 0, -4), (SEND, ZP, D0B, 0, -1), (SEND, ZP, D0, -1, 0), (WAIT, D0, 1, 2), (SEND, ZQ, D0, 1, 2),
+    (SEND, ZQ, D0, -1, 0), (PART, 1, 0, 1), (WAIT, SIB_D, 1, 1, 1), (WAIT, D1B, -1, 0), (PART, 1, 1, 1),
+    (WAIT, SIB_D, 1, -1, 1), (WAIT, D0B, -1, 2), (WAIT, D0, 0, -2), (SEND, ZP, D0, 0, -2), (WAIT, D0, 0, 3),
+    (PART, 1, -1, 1), (WAIT, SIB_D, 1, 0, 0), (WAIT, D1, -1, -2), (WAIT, D0B, 0, 3), (SEND, XQ, D0B, 0, 3),
+    (PART, 1, 0, 0), (WAIT, D0, 1, -1), (WAIT, D1, -1, 2), (WAIT, D0B, 0, -2), (SEND, XQ, D0B, 0, -2),
+    (SEND, XP, D0B, 0, -2), (SEND, ZP, D0B, 0, -2), (SEND, XP, D1B, 0, -4), (SEND, ZP, D0, 1, -1),
+    (SEND, XP, D0B, 0, 1), (SEND, XP, D0B, 0, -1), (SEND, XP, D0B, 0, 3), (SEND, XP, D0, -1, 0),
+    (WAIT, FAR, 1, 0, 1), (WAIT, D0, 1, 3), (SHARE_D, 1, 1, 0), (RELAY, 1, 0, 1), (WAIT, D1B, -1, 2),
+    (WAIT, FAR, 1, 1, 1), (WAIT, D0, -1, -1), (SEND, ZP, D0, -1, -1), (WAIT, D1B, -1, -2), (RELAY, 1, 1, 1),
+    (WAIT, D0, -1, 1), (SEND, ZQ, D0, -1, 1), (WAIT, SIB_D, 1, -1, 0), (WAIT, D1, -1, -4), (WAIT, FAR, 1, -1, 1),
+    (WAIT, D0, 0, -3), (SEND, ZP, D0, 0, -3), (WAIT, D0B, -1, -2), (RELAY, 1, -1, 1), (WAIT, D0B, 0, -3),
+    (SEND, XQ, D0B, 0, -3), (SEND, XP, D0B, 0, -3), (SEND, XP, D0B, -1, 0), (SEND, XP, D0B, -1, 2),
+    (SEND, XP, D0B, -1, -2), (SEND, ZP, D0B, 0, -3), (SEND, XP, D1, -1, -1), (SEND, XP, D1, -1, 1),
+    (SEND, XP, D1B, -1, -1), (SEND, XP, D1B, -1, 1), (SHARE_D, 0, 0, 1), (WAIT, D1B, -1, -4), (SHARE_D, 1, -1, 0),
+    (PART, 1, -1, 0), (WAIT, D0B, -1, 1), (WAIT, FAR, 1, 0, 0), (WAIT, D0, 1, -2), (SEND, ZP, D0, 1, -2),
+    (WAIT, D0B, -1, -1), (WAIT, D0B, -1, 3), (RELAY, 1, 0, 0), (FINAL, 1, 0, 1), (FINAL, 1, 1, 1),
+    (WAIT, SIB_D, 0, 0, 1), (PART, 0, 0, 1), (WAIT, D0, 2, 0), (SEND, ZP, D0, 2, 0), (SEND, ZQ, D0, 2, 0),
+    (WAIT, D0, -1, -2), (SEND, ZP, D0, -1, -2), (WAIT, D0B, -1, -3), (WAIT, SIB_D, 1, 1, 0), (WAIT, D0, -1, 2),
+    (SEND, ZQ, D0, -1, 2), (PART, 1, 1, 0), (WAIT, D0, 0, -4), (WAIT, D0B, 0, -4), (SEND, XQ, D0B, 0, -4),
+    (SEND, XP, D0B, 0, -4), (SEND, XP, D1, -1, 3), (SEND, XP, D1B, -1, 3), (SEND, XP, D1, -1, -3),
+    (SEND, XP, D1B, -1, -3), (SEND, XP, D1, -1, 0), (SHARE_D, 0, 0, 0), (FINAL, 1, -1, 1), (WAIT, FAR, 1, -1, 0),
+    (RELAY, 1, -1, 0), (WAIT, D0, 1, -3), (SEND, ZP, D0, 1, -3), (SHARE_D, 0, 1, 1), (FINAL, 1, 0, 0),
+    (WAIT, SIB_D, 0, 0, 0), (WAIT, FAR, 0, 0, 1), (RELAY, 0, 0, 1), (PART, 0, 0, 0), (WAIT, D0B, -1, -4),
+    (SEND, XP, D0B, -1, -4), (SEND, XP, D1B, -1, 0), (SEND, XP, D1, -1, -2), (SEND, XP, D1, -1, 2),
+    (SEND, XP, D1B, -1, 2), (SEND, XP, D1B, -1, -2), (SEND, XP, D1, -1, -4), (SEND, XP, D1B, -1, -4),
+    (SEND, XP, D0B, -1, 1), (SEND, XP, D0B, -1, -1), (SEND, XP, D0B, -1, 3), (SEND, XP, D0B, -1, -3),
+    (WAIT, D0, 2, -1), (SEND, ZP, D0, 2, -1), (WAIT, D0, 2, 1), (SEND, ZQ, D0, 2, 1), (WAIT, SIB_D, 0, -1, 1),
+    (WAIT, FAR, 1, 1, 0), (RELAY, 1, 1, 0), (FINAL, 1, -1, 0), (WAIT, D0, -1, -3), (SEND, ZP, D0, -1, -3),
+    (WAIT, D0, -1, 3), (SHARE_D, 0, -1, 1), (PART, 0, -1, 1), (SHARE_D, 1, 2, 1), (FINAL, 0, 0, 1),
+    (WAIT, D0, 1, -4), (SHARE_D, 0, 1, 0), (WAIT, FAR, 0, 0, 0), (RELAY, 0, 0, 0), (WAIT, SIB_D, 0, 1, 1),
+    (PART, 0, 1, 1), (WAIT, D0, 2, 2), (SEND, ZQ, D0, 2, 2), (WAIT, D0, 2, -2), (SEND, ZP, D0, 2, -2),
+    (WAIT, SIB_D, 1, 2, 1), (PART, 1, 2, 1), (WAIT, D0, -1, -4), (SHARE_D, 0, -1, 0), (FINAL, 1, 1, 0),
+    (WAIT, SIB_D, 0, -1, 0), (WAIT, FAR, 0, -1, 1), (RELAY, 0, -1, 1), (PART, 0, -1, 0), (FINAL, 0, 0, 0),
+    (SHARE_D, 1, 2, 0), (WAIT, SIB_D, 0, 1, 0), (PART, 0, 1, 0), (WAIT, FAR, 0, 1, 1), (WAIT, D0, 2, 3),
+    (WAIT, D0, 2, -3), (SEND, ZP, D0, 2, -3), (RELAY, 0, 1, 1), (SHARE_D, 0, 2, 1), (WAIT, FAR, 1, 2, 1),
+    (RELAY, 1, 2, 1), (WAIT, SIB_D, 1, 2, 0), (PART, 1, 2, 0), (WAIT, FAR, 0, -1, 0), (RELAY, 0, -1, 0),
+    (WAIT, SIB_D, 0, 2, 1), (PART, 0, 2, 1), (WAIT, D0, 2, -4), (SHARE_D, 0, 2, 0), (FINAL, 0, -1, 1),
+    (WAIT, FAR, 0, 1, 0), (RELAY, 0, 1, 0), (FINAL, 0, 1, 1), (WAIT, SIB_D, 0, 2, 0), (DIRECT, 0, 2, 0),
+    (WAIT, FAR, 1, 2, 0), (RELAY, 1, 2, 0), (WAIT, FAR, 0, 2, 1), (RELAY, 0, 2, 1), (FINAL, 1, 2, 1),
+    (FINAL, 0, -1, 0), (FINAL, 0, 1, 0), (LAST, 0, 2, 0), (FINAL, 1, 2, 0), (FINAL, 0, 2, 1),
 )
 
 ITEMS = [(h, dx, rp) for h in (0, 1) for dx in (0, -1, 1, 2) for rp in (0, 1)]
@@ -100,9 +132,9 @@
 
 
 def kernel(
-    tok, gain, nbias, up, upb, down, dbias, out,
-    X, N, U, UB, D, H, O, A0, A1, S1, S2, S3, RL, FP, FQ,
-    loc, wsend, wrecv, xsend, xrecv, bsend, brecv, sibs, sibr, ysend, yrecv, stored,
+    tok, gain_in, nbias_in, up, upb, down, dbias_in, out,
+    gain, nbias, dbias, X, N, U, UB, D, H, A0, A1, S1, S2, S3, RL, FP, FQ,
+    loc, wsend, wrecv, xsend, xrecv, bsend, brecv, sibs, sibr, ysend, yrecv,
 ):
     img, tp = lax.axis_index("img"), lax.axis_index("tp")
     c = lax.rem(img, 2)
@@ -134,7 +166,11 @@
         pltpu.make_async_copy(down.at[:, pl.ds(128, 128)], D.at[1, 0, 0, zhi, :, pl.ds(0, 128)], loc.at[3]),
         pltpu.make_async_copy(upb, UB.at[z], loc.at[4]),
     ]
-    for copy in copies:
+    late = [
+        pltpu.make_async_copy(src, dst, loc.at[5 + i])
+        for i, (src, dst) in enumerate(((gain_in, gain), (nbias_in, nbias), (dbias_in, dbias)))
+    ]
+    for copy in copies + late:
         copy.start()
     barrier = pltpu.get_barrier_semaphore()
     partners = [sibling, *link.values(), opposite]
@@ -243,6 +279,8 @@
                 sibling,
             )
         elif op == NORM:
+            for copy in late:
+                copy.wait()
 
             @pl.loop(0, 4)
             def _(r):
@@ -291,8 +329,7 @@
                 total = total + RL[i].astype(F32)
             for half, core in ((0, c), (1, 1 - c)):
                 cols = pl.ds(pl.multiple_of((block + core) * 256 + h * 128, 128), 128)
-                O[:, cols] = (total[:, half * 128 : half * 128 + 128] + dbias[:, cols]).astype(BF16)
-                pltpu.make_async_copy(O.at[:, cols], out.at[:, cols], stored.at[0]).start()
+                out[:, cols] = (total[:, half * 128 : half * 128 + 128] + dbias[:, cols]).astype(BF16)
 
     def left(ref, ssem):
         pltpu.make_async_remote_copy(
@@ -308,7 +345,6 @@
     left(U.at[:, :, :, 0], sibs.at[1])
     for i in range(3):
         left(FP, ysend.at[i])
-    pltpu.make_async_copy(O, out, stored.at[0]).wait()
 
 
 def on_device(patch_tokens, norm_gain, norm_bias, up_weight, up_bias, down_weight, down_bias):
@@ -317,21 +353,23 @@
     dma = pltpu.SemaphoreType.DMA
     return pl.pallas_call(
         kernel,
-        out_shape=jax.ShapeDtypeStruct((128, 4096), BF16),
-        in_specs=[hbm, vmem, vmem, hbm, hbm, hbm, vmem],
-        out_specs=hbm,
+        out_shape=pltpu.VMEM((128, 4096), BF16),
+        in_specs=[hbm] * 7,
+        out_specs=vmem,
         scratch_shapes=[
+            pltpu.VMEM((1, 1024), F32),
+            pltpu.VMEM((1, 1024), F32),
+            pltpu.VMEM((1, 4096), F32),
             pltpu.VMEM((4, 128, 1024), BF16),
             pltpu.VMEM((512, 1024), BF16),
             pltpu.VMEM((4, 4, 2, 2, 64, 512), BF16),
             pltpu.VMEM((8, 1, 512), F32),
             pltpu.VMEM((2, 4, 2, 4, 512, 256), BF16),
             pltpu.VMEM((512, 2048), BF16),
-            pltpu.VMEM((128, 4096), BF16),
             pltpu.VMEM((16, 128, 256), F32),
             pltpu.VMEM((16, 128, 256), F32),
             *[pltpu.VMEM((16, 128, 256), BF16)] * 6,
-            dma((5,)),
+            dma((8,)),
             dma((5 * len(PIECES),)),
             dma((len(ARRIVALS),)),
             dma((1,)),
@@ -342,19 +380,23 @@
             dma((24,)),
             dma((3,)),
             dma((32,)),
-            dma((1,)),
         ],
         compiler_params=pltpu.CompilerParams(
             collective_id=0, has_side_effects=True, vmem_limit_bytes=62 * 1024 * 1024
         ),
     )(
-        patch_tokens,
-        norm_gain.reshape(1, -1),
-        norm_bias.reshape(1, -1),
-        up_weight,
-        up_bias.reshape(1, -1),
-        down_weight,
-        down_bias.reshape(1, -1),
+        *(
+            pltpu.with_memory_space_constraint(v, pltpu.HBM)
+            for v in (
+                patch_tokens,
+                norm_gain.reshape(1, -1),
+                norm_bias.reshape(1, -1),
+                up_weight,
+                up_bias.reshape(1, -1),
+                down_weight,
+                down_bias.reshape(1, -1),
+            )
+        )
     )
 
 

time: 88.6 us -> 82.9 us (0.936)
  Pallas kernels: 86.1 us -> 81.9 us
  local copies, waits for them, and re-layouts: 2.29 us -> 0.97 us
    pallas_call x1, Pallas kernels: 86.1 us -> 81.9 us  [on_device(): pl.pallas_call(kernel, out_shape=pltpu.VMEM((128, 4096), BF16), in_specs=...]
    unnamed x1, local copies, waits for them, and re-layouts: 2.29 us -> 0.97 us
where the time goes in v3:
time: 82.9 us; the launch traced here: 82.8 us
  Pallas kernels  81.9 us (99%)
  local copies, waits for them, and re-layouts  0.97 us (1%)
    pallas_call x1, Pallas kernels, on_device(): pl.pallas_call(kernel, out_shape=pltpu.VMEM((128, 4096), BF16), in_specs=...  81.9 us

profile of v3, /device:TPU:1, one launch (start us, length us, event | category | flops | bytes accessed | tf_op | source)
XLA Modules:
  0.0 82.8 jit_solution(10827860824617688320)
XLA Ops:
  0.0 81.9 %shard_map.73 = bf16[128,4096]{1,0:T(8,128)(2,1)S(1)} custom-call(bf16[128,1024]{1,0:T(8,128)(2,1)} %tok.1, f32[1,1024]{1,0:T(1,128)} %bitcast.5, f32[1,1024]{1,0:T(1,128)} %bitcast.6, bf16[64,512]{1,0:T(8,128)(2,1)} %up.1, f32[1,512]{1,0:T(1,128)} %bitcast.7, bf16[512,256]{1,0:T(8,128)(2,1)} %down.1, f32[1,4096]{1,0:T(1,128)} %bitcast.4), custom_call_target="tpu_custom_call" | custom-call | tf_op jit(solution)/shard_map/pallas_call | solution.py:354
  81.9 1.0 %copy.9 = bf16[128,4096]{1,0:T(8,128)(2,1)} copy(bf16[128,4096]{1,0:T(8,128)(2,1)S(1)} %shard_map.73) | data formatting | bytes 2097152

commit v4 on v3

v4 whole, which is shorter than its diff:
```python
import jax
import jax.numpy as jnp
from jax import lax
from jax.experimental import pallas as pl
from jax.experimental.pallas import tpu as pltpu
from jax.sharding import PartitionSpec as P

MESH = pl.DeviceIdType.MESH
F32, BF16 = jnp.float32, jnp.bfloat16

WAIT, SEND, SHARE_U, SHARE_D, NORM, HIDDEN, PART, DIRECT, RELAY, FINAL, LAST = range(11)
XP, XQ, YP, YQ, ZP, ZQ = range(6)
TOK, SIB_D, FAR = range(-3, 0)

WUA, WUB, D0, D0B, D1, D1B = range(6)
PIECES = ((None, 0, 32), (None, 32, 32), (0, 0, 384), (0, 384, 128), (1, 0, 256), (1, 256, 256))
BIASED = WUB
FROM_X = (WUA, D0,)

STEPS = (
    (SEND, XP, WUA, 0, 0), (SEND, XQ, WUA, 0, 0), (SEND, YP, TOK, 0), (SEND, YQ, TOK, 0), (SEND, ZP, WUA, 0, 0),
    (SEND, ZQ, WUA, 0, 0), (SEND, XP, D0B, 0, 0), (SEND, XQ, WUB, 0, 0), (SEND, ZP, WUB, 0, 0),
    (SEND, ZQ, WUB, 0, 0), (SEND, XP, D0, 0, 0), (SEND, XQ, D0, 0, 0), (SEND, ZP, D1, 0, 0), (SEND, ZQ, D1, 0, 0),
    (SEND, ZP, D1B, 0, 0), (SEND, ZQ, D1B, 0, 0), (SEND, XP, WUB, 0, 0), (SEND, XQ, D0B, 0, 0), (WAIT, WUA, -1, 0),
    (WAIT, WUA, 1, 0), (SEND, ZP, WUA, 1, 0), (SEND, ZQ, WUA, 1, 0), (SEND, ZP, WUA, -1, 0), (SEND, ZQ, WUA, -1, 0),
    (WAIT, WUA, 0, -1), (WAIT, WUA, 0, 1), (WAIT, D0B, -1, 0), (WAIT, WUB, 0, -1), (SEND, XP, WUB, 0, -1),
    (SEND, XQ, WUB, 0, -1), (SEND, ZP, WUB, 0, -1), (SEND, ZP, WUA, 0, -1), (WAIT, WUB, 0, 1), (SEND, XP, WUB, 0, 1),
    (SEND, XQ, WUB, 0, 1), (SEND, XP, WUA, -1, 0), (SEND, ZQ, WUB, 0, 1), (SEND, ZQ, WUA, 0, 1), (WAIT, D1, 0, -1),
    (SEND, XQ, D1, 0, -1), (SEND, XP, D1, 0, -1), (SEND, ZP, D1, 0, -1), (WAIT, D1, 0, 1), (SEND, XQ, D1, 0, 1),
    (SEND, ZQ, D1, 0, 1), (WAIT, D0, -1, 0), (WAIT, D0, 1, 0), (WAIT, WUB, -1, 0), (WAIT, D1B, 0, -1),
    (SEND, XQ, D1B, 0, -1), (WAIT, D1B, 0, 1), (WAIT, WUB, -1, -1), (SEND, XP, WUB, -1, -1), (WAIT, WUA, 1, -1),
    (SEND, ZP, WUA, 1, -1), (WAIT, WUA, 1, 1), (SEND, ZQ, WUA, 1, 1), (WAIT, WUB, -1, 1), (SEND, XP, WUB, -1, 1),
    (WAIT, TOK, -1), (SEND, YP, TOK, -1), (WAIT, TOK, 1), (WAIT, WUA, -1, -1), (WAIT, WUA, -1, 1), (WAIT, WUA, 2, 0),
    (WAIT, WUB, 0, -2), (SEND, XP, WUB, 0, -2), (SEND, ZP, WUB, 0, -2), (SEND, XQ, WUB, 0, -2), (WAIT, WUB, 0, 2),
    (SEND, ZQ, WUB, 0, 2), (SEND, XP, WUB, 0, 2), (SEND, XP, WUB, -1, 0), (SEND, XQ, WUB, 0, 2),
    (SEND, XP, D1, 0, 1), (SEND, XQ, D1B, 0, 1), (WAIT, WUA, 0, -2), (SEND, ZP, WUA, 0, -2), (SEND, ZP, WUA, 2, 0),
    (SEND, ZP, WUA, -1, -1), (WAIT, WUA, 0, 2), (SEND, ZQ, WUA, 0, 2), (SEND, ZQ, WUA, 2, 0), (SEND, ZQ, WUA, -1, 1),
    (WAIT, D1, -1, -1), (WAIT, D1, 0, -2), (WAIT, D1, 0, 2), (WAIT, WUA, 1, -2), (SEND, ZP, WUA, 1, -2),
    (WAIT, WUA, 1, 2), (SEND, ZQ, WUA, 1, 2), (SEND, ZQ, D1B, 0, 1), (SEND, ZQ, D1, 0, 2), (WAIT, WUB, -1, -2),
    (WAIT, WUB, 0, -3), (SEND, XP, WUB, 0, -3), (SEND, XQ, WUB, 0, -3), (SEND, ZP, WUB, 0, -3), (WAIT, WUB, 0, 3),
    (SEND, XQ, WUB, 0, 3), (SEND, XP, WUB, 0, 3), (SEND, XP, WUB, -1, -2), (SEND, XQ, D1B, 0, 0),
    (SEND, XQ, D1, 0, -2), (WAIT, WUB, -1, 2), (SEND, XP, WUB, -1, 2), (SEND, XP, D1B, 0, -1), (WAIT, WUA, 0, -3),
    (SEND, ZP, WUA, 0, -3), (SEND, ZP, D1B, 0, -1), (WAIT, WUA, 0, 3), (WAIT, TOK, 2), (NORM,), (WAIT, WUA, 2, -1),
    (WAIT, WUA, 2, 1), (WAIT, WUA, -1, -2), (SEND, ZP, WUA, -1, -2), (WAIT, WUA, -1, 2), (SEND, ZQ, WUA, -1, 2),
    (SEND, ZQ, WUA, 2, 1), (SHARE_U, 0), (SHARE_U, -1), (SHARE_U, 1), (WAIT, D1, -1, 1), (WAIT, WUA, 1, -3),
    (SEND, ZP, WUA, 1, -3), (SEND, ZP, WUA, 2, -1), (SEND, ZP, D1, 0, -2), (WAIT, WUA, 1, 3), (WAIT, WUB, -1, -3),
    (SEND, XP, WUB, -1, -3), (WAIT, WUB, 0, -4), (SEND, XQ, WUB, 0, -4), (SEND, XQ, D1, 0, 2), (WAIT, WUB, -1, 3),
    (SEND, XP, WUB, -1, 3), (SEND, XP, WUB, 0, -4), (WAIT, WUA, 0, -4), (WAIT, D1B, 0, 2), (SEND, ZQ, D1B, 0, 2),
    (SEND, ZQ, D0, 0, 0), (SEND, XP, D1B, 0, 2), (SEND, XP, D1B, 0, 1), (HIDDEN, 0), (WAIT, D1B, 0, -2),
    (WAIT, D1, 0, 3), (SEND, XQ, D1, 0, 3), (SEND, XQ, D1B, 0, -2), (WAIT, WUA, -1, -3), (SEND, ZP, WUA, -1, -3),
    (SEND, ZP, D1B, 0, -2), (WAIT, WUA, -1, 3), (WAIT, D1B, -1, -1), (WAIT, WUA, 1, -4), (WAIT, WUA, 2, 2),
    (SEND, ZQ, WUA, 2, 2), (SEND, ZQ, D0B, 0, 0), (SEND, ZQ, D0, 1, 0), (SHARE_U, 2), (WAIT, WUA, 2, -2),
    (SEND, ZP, WUA, 2, -2), (SHARE_U, -2), (WAIT, D1B, 0, 3), (SEND, XQ, D1B, 0, 3), (WAIT, WUB, -1, -4),
    (SEND, XP, WUB, -1, -4), (SEND, XP, D1, 0, 3), (SEND, XP, D1B, 0, 3), (WAIT, D1, 0, -3), (SEND, ZP, D1, 0, -3),
    (SEND, XQ, D1, 0, -3), (SEND, ZP, D0, 0, 0), (SEND, XP, D1, 0, -3), (HIDDEN, 1), (WAIT, WUA, -1, -4),
    (WAIT, D1B, -1, 2), (WAIT, D0, 0, 1), (SEND, ZQ, D0, 0, 1), (WAIT, D1B, 0, -3), (SEND, XQ, D1B, 0, -3),
    (SEND, XP, D1B, 0, -3), (SEND, XP, D1, 0, 0), (WAIT, WUA, 2, 3), (SHARE_D, 1, 0, 1), (SHARE_U, 3),
    (WAIT, D1B, -1, 1), (WAIT, WUA, 2, -3), (SEND, ZP, WUA, 2, -3), (SEND, ZP, D1B, 0, -3), (SEND, ZP, D0B, 0, 0),
    (WAIT, D0B, 0, 1), (SEND, ZQ, D0B, 0, 1), (SHARE_U, -3), (WAIT, D1, 0, -4), (SEND, XQ, D1, 0, -4),
    (SEND, XQ, D0B, 0, 1), (SEND, XQ, D1B, 0, 2), (WAIT, SIB_D, 1, 0, 1), (WAIT, D1, -1, 3), (WAIT, D0, 1, 1),
    (SEND, ZQ, D0, 1, 1), (HIDDEN, 2), (WAIT, D1B, -1, 3), (WAIT, D0, 0, -1), (SEND, ZP, D0, 0, -1),
    (SEND, ZP, D0, 1, 0), (WAIT, WUA, 2, -4), (WAIT, D0, 0, 2), (SEND, ZQ, D0, 0, 2), (SHARE_D, 1, 1, 1),
    (SHARE_U, -4), (WAIT, D1, -1, -3), (WAIT, D0B, 0, 2), (SEND, XQ, D0B, 0, 2), (SEND, XP, D0B, 0, 2),
    (SEND, XP, D1B, 0, 0), (SEND, ZQ, D0B, 0, 2), (SEND, XP, D1, 0, -2), (SEND, XP, D1, 0, 2),
    (SEND, XP, D1B, 0, -2), (SEND, XP, D1, 0, -4), (WAIT, D1B, 0, -4), (SEND, XQ, D1B, 0, -4),
    (SEND, XP, D1B, 0, -4), (SHARE_D, 1, 0, 0), (WAIT, D1B, -1, -3), (WAIT, D0B, 0, -1), (SEND, XQ, D0B, 0, -1),
    (SEND, XQ, D1, 0, 0), (SEND, ZP, D0B, 0, -1), (SEND, ZP, D0, -1, 0), (SHARE_D, 1, -1, 1),
    (WAIT, SIB_D, 1, -1, 1), (WAIT, D0, 1, 2), (SEND, ZQ, D0, 1, 2), (SEND, ZQ, D0, -1, 0), (HIDDEN, 3),
    (WAIT, D1, -1, 0), (WAIT, SIB_D, 1, 0, 0), (PART, 1, 0, 1), (WAIT, D0B, -1, 2), (WAIT, D0, 0, -2),
    (SEND, ZP, D0, 0, -2), (WAIT, SIB_D, 1, 1, 1), (PART, 1, -1, 1), (WAIT, D1B, -1, 0), (WAIT, D0B, 0, 3),
    (SEND, XQ, D0B, 0, 3), (PART, 1, 0, 0), (WAIT, D0, 1, -1), (SEND, ZP, D0, 1, -1), (PART, 1, 1, 1),
    (WAIT, D1, -1, -2), (WAIT, D0B, 0, -2), (SEND, XQ, D0B, 0, -2), (SEND, XP, D0B, 0, -2), (SEND, XP, D0B, 0, 1),
    (SEND, ZP, D0B, 0, -2), (SEND, XP, D0B, 0, -1), (SEND, XP, D0B, -1, 0), (SEND, XP, D0, -1, 0),
    (SEND, XP, D0B, 0, 3), (SEND, XP, D1, -1, -1), (SHARE_D, 1, 1, 0), (WAIT, D1, -1, 2), (WAIT, FAR, 1, 0, 1),
    (RELAY, 1, 0, 1), (WAIT, D0, -1, -1), (SEND, ZP, D0, -1, -1), (WAIT, D1B, -1, -2), (WAIT, D0, -1, 1),
    (SEND, ZQ, D0, -1, 1), (WAIT, D1, -1, -4), (WAIT, FAR, 1, -1, 1), (RELAY, 1, -1, 1), (WAIT, SIB_D, 1, -1, 0),
    (WAIT, D0, 0, -3), (SEND, ZP, D0, 0, -3), (WAIT, D1B, -1, -4), (SHARE_D, 1, -1, 0), (PART, 1, -1, 0),
    (WAIT, D0B, -1, -2), (WAIT, FAR, 1, 0, 0), (WAIT, D0, 1, -2), (WAIT, D0B, -1, 1), (WAIT, D0B, 0, -3),
    (SEND, XP, D0B, 0, -3), (SEND, XQ, D0B, 0, -3), (SEND, ZP, D0B, 0, -3), (SEND, XP, D1, -1, 1),
    (SEND, ZP, D0, 1, -2), (SEND, XP, D1B, -1, -1), (SEND, XP, D1B, -1, 1), (SEND, XP, D1, -1, 3),
    (WAIT, D0B, -1, -1), (SHARE_D, 0, 0, 1), (RELAY, 1, 0, 0), (WAIT, FAR, 1, 1, 1), (RELAY, 1, 1, 1),
    (WAIT, SIB_D, 1, 1, 0), (WAIT, D0, 2, 0), (SEND, ZQ, D0, 2, 0), (PART, 1, 1, 0), (WAIT, D0B, -1, 3),
    (WAIT, D0, -1, -2), (SEND, ZP, D0, -1, -2), (SEND, ZP, D0, 2, 0), (WAIT, D0, -1, 2), (SEND, ZQ, D0, -1, 2),
    (WAIT, SIB_D, 0, 0, 1), (PART, 0, 0, 1), (WAIT, D0B, -1, -3), (WAIT, D0B, 0, -4), (SEND, XQ, D0B, 0, -4),
    (SEND, XP, D0B, 0, -4), (SEND, XP, D1B, -1, 3), (SEND, XP, D1, -1, -3), (SEND, XP, D1B, -1, -3),
    (SEND, XP, D0B, -1, 2), (SEND, XP, D0B, -1, -2), (SEND, XP, D1, -1, 0), (SEND, XP, D1B, -1, 0),
    (SEND, XP, D1B, -1, 2), (SEND, XP, D1, -1, -2), (SEND, XP, D1, -1, 2), (SEND, XP, D1B, -1, -2),
    (SEND, XP, D1, -1, -4), (SEND, XP, D1B, -1, -4), (SHARE_D, 0, 0, 0), (FINAL, 1, 0, 1), (WAIT, FAR, 1, -1, 0),
    (RELAY, 1, -1, 0), (FINAL, 1, -1, 1), (FINAL, 1, 0, 0), (WAIT, D0, 1, -3), (SEND, ZP, D0, 1, -3),
    (SHARE_D, 0, 1, 1), (FINAL, 1, 1, 1), (WAIT, SIB_D, 0, 0, 0), (WAIT, D0, 2, 1), (SEND, ZQ, D0, 2, 1),
    (PART, 0, 0, 0), (WAIT, D0B, -1, -4), (SEND, XP, D0B, -1, -4), (SEND, XP, D0B, -1, 1), (SEND, XP, D0B, -1, -1),
    (SEND, XP, D0B, -1, 3), (SEND, XP, D0B, -1, -3), (WAIT, FAR, 1, 1, 0), (RELAY, 1, 1, 0), (WAIT, D0, -1, -3),
    (SEND, ZP, D0, -1, -3), (WAIT, SIB_D, 0, -1, 1), (WAIT, FAR, 0, 0, 1), (RELAY, 0, 0, 1), (SHARE_D, 0, -1, 1),
    (PART, 0, -1, 1), (WAIT, D0, 2, -1), (SEND, ZP, D0, 2, -1), (SHARE_D, 1, 2, 1), (FINAL, 1, -1, 0),
    (WAIT, D0, 2, 2), (SEND, ZQ, D0, 2, 2), (WAIT, SIB_D, 0, 1, 1), (WAIT, FAR, 0, 0, 0), (RELAY, 0, 0, 0),
    (SHARE_D, 0, 1, 0), (PART, 0, 1, 1), (WAIT, SIB_D, 1, 2, 1), (SHARE_D, 0, -1, 0), (PART, 1, 2, 1),
    (FINAL, 1, 1, 0), (WAIT, D0, 2, -2), (SEND, ZP, D0, 2, -2), (FINAL, 0, 0, 1), (WAIT, SIB_D, 0, -1, 0),
    (PART, 0, -1, 0), (WAIT, FAR, 0, -1, 1), (WAIT, SIB_D, 0, 1, 0), (RELAY, 0, -1, 1), (PART, 0, 1, 0),
    (SHARE_D, 1, 2, 0), (FINAL, 0, 0, 0), (WAIT, FAR, 0, 1, 1), (RELAY, 0, 1, 1), (WAIT, D0, 2, -3),
    (SEND, ZP, D0, 2, -3), (SHARE_D, 0, 2, 1), (WAIT, FAR, 1, 2, 1), (RELAY, 1, 2, 1), (WAIT, SIB_D, 1, 2, 0),
    (PART, 1, 2, 0), (WAIT, FAR, 0, -1, 0), (RELAY, 0, -1, 0), (WAIT, SIB_D, 0, 2, 1), (PART, 0, 2, 1),
    (WAIT, FAR, 0, 1, 0), (SHARE_D, 0, 2, 0), (RELAY, 0, 1, 0), (FINAL, 0, -1, 1), (FINAL, 0, 1, 1),
    (WAIT, SIB_D, 0, 2, 0), (WAIT, FAR, 1, 2, 0), (RELAY, 1, 2, 0), (DIRECT, 0, 2, 0), (WAIT, FAR, 0, 2, 1),
    (RELAY, 0, 2, 1), (FINAL, 1, 2, 1), (FINAL, 0, -1, 0), (FINAL, 0, 1, 0), (FINAL, 1, 2, 0), (LAST, 0, 2, 0),
    (FINAL, 0, 2, 1),
)

ITEMS = [(h, dx, rp) for h in (0, 1) for dx in (0, -1, 1, 2) for rp in (0, 1)]
OFFSETS = (0, -1, 1, -2, 2, -3, 3, -4)
AFTER = {XP: -1, XQ: 1, YP: -1, YQ: 1, ZP: -1, ZQ: 1}


def slot(dx):
    return dx % 4


def rows_of(half, from_x):
    return sum(PIECES[k][2] for k in range(len(PIECES)) if PIECES[k][0] == half and (k in FROM_X) == from_x)


def arrival(kind, dx, dz):
    half, from_x = PIECES[kind][0], kind in FROM_X
    if half is None:
        return (1, kind, dz, 0) if not from_x and dx in (1, 2) else (0, kind, dx, dz)
    if from_x:
        return (3, half, dx, dz) if dz in (3, -4) else (0, kind, dx, dz)
    return (2, half, dx, dz % 2) if dx in (1, 2) else (0, kind, dx, dz)


ARRIVALS = sorted({arrival(k, dx, dz) for k in range(len(PIECES)) for dx in (0, -1, 1, 2) for dz in OFFSETS if dx or dz})

SIZES = sorted({(half is None, rows) for half, _, rows in PIECES})
GROUPS = [
    (size, power)
    for size in SIZES
    for power in range(7)
    if 31 * sum((half is None, rows) == size for half, _, rows in PIECES) >> power & 1
]
LEAVE = {size: [GROUPS.index((s, p)) for s, p in GROUPS if s == size for _ in range(2**p)] for size in SIZES}


def kernel(
    tok, gain_in, nbias_in, up, upb, down, dbias_in, out,
    gain, nbias, dbias, X, N, U, UB, D, H, A0, A1, S1, S2, S3, RL, FP, FQ,
    loc, wsend, wrecv, xsend, xrecv, bsend, brecv, sibs, sibr, ysend, yrecv,
):
    img, tp = lax.axis_index("img"), lax.axis_index("tp")
    c = lax.rem(img, 2)
    zlo = lax.rem(img // 2, 2)
    x = img // 4
    zhi = lax.rem(tp, 4)
    y = tp // 4
    z = zhi * 2 + zlo
    sign = 1 - 2 * c

    def wrap(v, n):
        return lax.rem(v + 2 * n, n)

    def at(dx=0, dy=0, dz=0, core=None):
        xx, yy, zz = wrap(x + sign * dx, 4), wrap(y + sign * dy, 4), wrap(z + sign * dz, 8)
        cc = c if core is None else core
        return {"img": xx * 4 + lax.rem(zz, 2) * 2 + cc, "tp": yy * 4 + zz // 2}

    sibling = at(core=1 - c)
    opposite = at(dy=2)
    link = {
        XP: at(dx=1), XQ: at(dx=-1), YP: at(dy=1), YQ: at(dy=-1), ZP: at(dz=1), ZQ: at(dz=-1),
    }

    copies = [
        pltpu.make_async_copy(tok, X.at[0], loc.at[0]),
        pltpu.make_async_copy(up, U.at[zhi, x, zlo, c], loc.at[1]),
        pltpu.make_async_copy(down.at[:, pl.ds(0, 128)], D.at[0, 0, 0, zhi, :, pl.ds(0, 128)], loc.at[2]),
        pltpu.make_async_copy(down.at[:, pl.ds(128, 128)], D.at[1, 0, 0, zhi, :, pl.ds(0, 128)], loc.at[3]),
        pltpu.make_async_copy(upb, UB.at[z], loc.at[4]),
    ]
    late = [
        pltpu.make_async_copy(src, dst, loc.at[5 + i])
        for i, (src, dst) in enumerate(((gain_in, gain), (nbias_in, nbias), (dbias_in, dbias)))
    ]
    for copy in copies + late:
        copy.start()
    barrier = pltpu.get_barrier_semaphore()
    partners = [sibling, *link.values(), opposite]
    for device in partners:
        pl.semaphore_signal(barrier, inc=1, device_id=device, device_id_type=MESH)
    pl.semaphore_wait(barrier, len(partners))
    for copy in copies:
        copy.wait()

    def send(src, dst, ssem, rsem, device):
        pltpu.make_async_remote_copy(
            src_ref=src, dst_ref=dst, send_sem=ssem, recv_sem=rsem, device_id=device, device_id_type=MESH
        ).start()

    def arrive(ref, rsem):
        pltpu.make_async_remote_copy(
            src_ref=ref, dst_ref=ref, send_sem=rsem, recv_sem=rsem, device_id=sibling, device_id_type=MESH
        ).wait_recv()

    def where(kind, dx, dz, dx_there=None, dz_there=None):
        half, row, rows = PIECES[kind]
        zz = wrap(z + sign * dz, 8)
        if half is None:
            return U.at[zz // 2, wrap(x + sign * dx, 4), lax.rem(zz, 2), c, pl.ds(row, rows)]
        dx_there = dx if dx_there is None else dx_there
        dz_there = dz if dz_there is None else dz_there
        return D.at[half, slot(dx_there), dz_there % 2, zz // 2, pl.ds(row, rows), pl.ds(0, 128)]

    def some(size, power):
        if size[0]:
            v = U.at[:, :, :, :, pl.ds(0, size[1])]
            return (v.at[0, 0, 0, 0], v.at[0, 0, 0], v.at[0, 0], v.at[0, 0:2], v.at[0], v.at[0:2], v)[power]
        v = D.at[:, :, :, :, pl.ds(0, size[1]), pl.ds(0, 128)]
        return (v.at[0, 0, 0, 0], v.at[0, 0, 0, 0:2], v.at[0, 0, 0], v.at[0, 0], v.at[0, 0:2], v.at[0], v)[power]

    leaving = {size: list(groups) for size, groups in LEAVE.items()}
    used = [0]

    def forward(path, kind, dx, dz):
        step = AFTER[path]
        dx_there, dz_there = (dx + step, dz) if path in (XP, XQ) else (dx, dz + step)
        dx_there = 2 if dx_there == -2 else dx_there
        send(
            where(kind, dx, dz),
            where(kind, dx, dz, dx_there, dz_there),
            wsend.at[leaving[(PIECES[kind][0] is None, PIECES[kind][2])].pop()],
            wrecv.at[ARRIVALS.index(arrival(kind, dx_there, dz_there))],
            link[path],
        )
        if kind == BIASED and path in (ZP, ZQ):
            bias = UB.at[wrap(z + sign * dz, 8)]
            send(bias, bias, bsend.at[0], brecv.at[dz_there % 8], link[path])

    def forward_tokens(path, dy):
        there = slot(dy + AFTER[path])
        send(X.at[slot(dy)], X.at[there], xsend.at[0], xrecv.at[there - 1], link[path])

    def send_y(src, dst, rsem, device):
        send(src, dst, ysend.at[used[0] // 16], rsem, device)
        used[0] += 1

    for step in STEPS:
        op, args = step[0], step[1:]
        if op == SEND:
            if args[1] == TOK:
                forward_tokens(args[0], args[2])
            else:
                forward(*args)
        elif op == WAIT:
            kind = args[0]
            if kind == TOK:
                arrive(X.at[slot(args[1])], xrecv.at[slot(args[1]) - 1])
            elif kind >= 0:
                arrive(where(*args), wrecv.at[ARRIVALS.index(arrival(*args))])
                if kind == BIASED and args[1] == 0:
                    arrive(UB.at[wrap(z + sign * args[2], 8)], brecv.at[args[2] % 8])
            elif kind == SIB_D:
                h, dx, rp = args[1:]
                arrive(D.at[h, slot(dx), rp, :, :, pl.ds(128, 128)], sibr.at[ITEMS.index((h, dx, rp))])
            else:
                i = ITEMS.index(args[1:])
                arrive(RL.at[i], yrecv.at[i])
        elif op == SHARE_U:
            dz = args[0]
            zz = wrap(z + sign * dz, 8)
            block = U.at[zz // 2, :, lax.rem(zz, 2), c]
            for kind, (half, _, _) in enumerate(PIECES):
                if half is None and kind not in FROM_X:
                    arrive(some((True, PIECES[kind][2]), 1), wrecv.at[ARRIVALS.index(arrival(kind, 1, dz))])
            send(block, block, sibs.at[1], sibr.at[16 + max(abs(dz) - 1, 0)], sibling)
        elif op == SHARE_D:
            h, dx, rp = args
            there = ITEMS.index((h, -dx if dx in (-1, 1) else dx, rp))
            if rows_of(h, False) and dx in (1, 2):
                block = D.at[0, 0, 0, :, pl.ds(0, rows_of(h, False)), pl.ds(0, 128)]
                arrive(block, wrecv.at[ARRIVALS.index((2, h, dx, rp))])
            if rows_of(h, True):
                block = D.at[0, 0, 0, 0, pl.ds(0, rows_of(h, True)), pl.ds(0, 128)]
                arrive(block, wrecv.at[ARRIVALS.index((3, h, dx, 3 if rp else -4))])
            send(
                D.at[h, slot(dx), rp, :, :, pl.ds(0, 128)],
                D.at[h, slot(-dx), rp, :, :, pl.ds(128, 128)],
                sibs.at[0],
                sibr.at[there],
                sibling,
            )
        elif op == NORM:
            for copy in late:
                copy.wait()

            @pl.loop(0, 4)
            def _(r):
                values = X[r].astype(F32)
                center = jnp.mean(values, axis=1, keepdims=True)
                spread = jnp.mean((values - center) ** 2, axis=1, keepdims=True)
                rows = (values - center) * lax.rsqrt(spread + 1e-05) * gain[...] + nbias[...]
                N[pl.ds(pl.multiple_of(r * 128, 128), 128), :] = rows.astype(BF16)

        elif op == HIDDEN:
            arrive(U.at[0 : (3, 2, 2, 1)[args[0]], :, 0, 0], sibr.at[16 + args[0]])
            side = 1 - 2 * zlo
            zz = wrap(z + (0, -2 * side, 2 * side, 4)[args[0]], 8)
            g = zz // 2
            summed = jnp.dot(N[...], U[g].reshape(1024, 512), preferred_element_type=F32)
            hidden = jax.nn.gelu(summed + UB[zz], approximate=True)
            H[:, pl.ds(pl.multiple_of(g * 512, 512), 512)] = hidden.astype(BF16)

        elif op in (PART, DIRECT):
            h, dx, rp = args
            i = ITEMS.index(args)
            columns = D[h, slot(dx), rp].reshape(2048, 256)
            here, there = (jnp.dot(H[m : m + 256], columns, preferred_element_type=F32) for m in (0, 256))
            A0[i] = here[0:128]
            S2[i] = there[0:128].astype(BF16)
            S3[i] = there[128:256].astype(BF16)
            if op == PART:
                A1[i] = here[128:256]
                send_y(S2.at[i], RL.at[i], yrecv.at[i], link[YP])
                send_y(S3.at[i], FP.at[i], yrecv.at[16 + i], link[YQ])
            else:
                S1[i] = here[128:256].astype(BF16)
                send_y(S2.at[i], RL.at[i], yrecv.at[16 + i], opposite)
                send_y(S3.at[i], FP.at[i], yrecv.at[16 + i], link[YQ])
                send_y(S1.at[i], FQ.at[i], yrecv.at[16 + i], link[YP])
        elif op == RELAY:
            i = ITEMS.index(args)
            S1[i] = (A1[i] + RL[i].astype(F32)).astype(BF16)
            send_y(S1.at[i], FQ.at[i], yrecv.at[16 + i], link[YP])
        elif op in (FINAL, LAST):
            h, dx, rp = args
            i = ITEMS.index(args)
            block = wrap(x + sign * dx, 4) * 4 + lax.rem(zlo + rp, 2) * 2
            arrive(FP.at[0 : 2 if op == FINAL else 3], yrecv.at[16 + i])
            total = A0[i] + FP[i].astype(F32) + FQ[i].astype(F32)
            if op == LAST:
                total = total + RL[i].astype(F32)
            for half, core in ((0, c), (1, 1 - c)):
                cols = pl.ds(pl.multiple_of((block + core) * 256 + h * 128, 128), 128)
                out[:, cols] = (total[:, half * 128 : half * 128 + 128] + dbias[:, cols]).astype(BF16)

    def left(ref, ssem):
        pltpu.make_async_remote_copy(
            src_ref=ref, dst_ref=ref, send_sem=ssem, recv_sem=ssem, device_id=sibling, device_id_type=MESH
        ).wait_send()

    left(X.at[0:3], xsend.at[0])
    left(UB.at[0:7], bsend.at[0])
    for i, group in enumerate(GROUPS):
        left(some(*group), wsend.at[i])
    left(D.at[:, :, :, :, :, pl.ds(0, 128)], sibs.at[0])
    left(U.at[:, :, :, 0], sibs.at[1])
    for i in range(3):
        left(FP, ysend.at[i])


def on_device(patch_tokens, norm_gain, norm_bias, up_weight, up_bias, down_weight, down_bias):
    hbm = pl.BlockSpec(memory_space=pltpu.HBM)
    vmem = pl.BlockSpec(memory_space=pltpu.VMEM)
    dma = pltpu.SemaphoreType.DMA
    return pl.pallas_call(
        kernel,
        out_shape=pltpu.VMEM((128, 4096), BF16),
        in_specs=[hbm] * 7,
        out_specs=vmem,
        scratch_shapes=[
            pltpu.VMEM((1, 1024), F32),
            pltpu.VMEM((1, 1024), F32),
            pltpu.VMEM((1, 4096), F32),
            pltpu.VMEM((4, 128, 1024), BF16),
            pltpu.VMEM((512, 1024), BF16),
            pltpu.VMEM((4, 4, 2, 2, 64, 512), BF16),
            pltpu.VMEM((8, 1, 512), F32),
            pltpu.VMEM((2, 4, 2, 4, 512, 256), BF16),
            pltpu.VMEM((512, 2048), BF16),
            pltpu.VMEM((16, 128, 256), F32),
            pltpu.VMEM((16, 128, 256), F32),
            *[pltpu.VMEM((16, 128, 256), BF16)] * 6,
            dma((8,)),
            dma((len(GROUPS),)),
            dma((len(ARRIVALS),)),
            dma((1,)),
            dma((3,)),
            dma((1,)),
            dma((8,)),
            dma((2,)),
            dma((20,)),
            dma((3,)),
            dma((32,)),
        ],
        compiler_params=pltpu.CompilerParams(
            collective_id=0, has_side_effects=True, vmem_limit_bytes=62 * 1024 * 1024
        ),
    )(
        *(
            pltpu.with_memory_space_constraint(v, pltpu.HBM)
            for v in (
                patch_tokens,
                norm_gain.reshape(1, -1),
                norm_bias.reshape(1, -1),
                up_weight,
                up_bias.reshape(1, -1),
                down_weight,
                down_bias.reshape(1, -1),
            )
        )
    )


def solution(mesh):
    return jax.shard_map(
        on_device,
        mesh=mesh,
        in_specs=(P(("img", "tp"), None), P(), P(), P("img", "tp"), P("tp"), P("tp", "img"), P()),
        out_specs=P(("img", "tp"), None),
        check_vma=False,
    )
```

time: 82.9 us -> 82.2 us (level)
  no operation moved by 1% of the time
where the time goes in v4:
time: 82.2 us; the launch traced here: 82.1 us
  Pallas kernels  81.1 us (99%)
  local copies, waits for them, and re-layouts  0.97 us (1%)
    pallas_call x1, Pallas kernels, on_device(): pl.pallas_call(kernel, out_shape=pltpu.VMEM((128, 4096), BF16), in_specs=...  81.1 us

profile of v4, /device:TPU:1, one launch (start us, length us, event | category | flops | bytes accessed | tf_op | source)
XLA Modules:
  0.0 82.1 jit_solution(14958875219610565374)
XLA Ops:
  0.0 81.1 %shard_map.73 = bf16[128,4096]{1,0:T(8,128)(2,1)S(1)} custom-call(bf16[128,1024]{1,0:T(8,128)(2,1)} %tok.1, f32[1,1024]{1,0:T(1,128)} %bitcast.5, f32[1,1024]{1,0:T(1,128)} %bitcast.6, bf16[64,512]{1,0:T(8,128)(2,1)} %up.1, f32[1,512]{1,0:T(1,128)} %bitcast.7, bf16[512,256]{1,0:T(8,128)(2,1)} %down.1, f32[1,4096]{1,0:T(1,128)} %bitcast.4), custom_call_target="tpu_custom_call" | custom-call | tf_op jit(solution)/shard_map/pallas_call | solution.py:361
  81.1 1.0 %copy.9 = bf16[128,4096]{1,0:T(8,128)(2,1)} copy(bf16[128,4096]{1,0:T(8,128)(2,1)S(1)} %shard_map.73) | data formatting | bytes 2097152

commit v5 on v4

--- a/solution.py
+++ b/solution.py
@@ -232,6 +232,18 @@
             bias = UB.at[wrap(z + sign * dz, 8)]
             send(bias, bias, bsend.at[0], brecv.at[dz_there % 8], link[path])
 
+    def share(kind, dx, dz):
+        half, row, rows = PIECES[kind]
+        zz = wrap(z + sign * dz, 8)
+        there = (half, -dx if dx in (-1, 1) else dx, dz % 2)
+        send(
+            D.at[half, slot(dx), dz % 2, zz // 2, pl.ds(row, rows), pl.ds(0, 128)],
+            D.at[half, slot(-dx), dz % 2, zz // 2, pl.ds(row, rows), pl.ds(128, 128)],
+            sibs.at[0],
+            sibr.at[ITEMS.index(there)],
+            sibling,
+        )
+
     def forward_tokens(path, dy):
         there = slot(dy + AFTER[path])
         send(X.at[slot(dy)], X.at[there], xsend.at[0], xrecv.at[there - 1], link[path])
@@ -253,6 +265,8 @@
                 arrive(X.at[slot(args[1])], xrecv.at[slot(args[1]) - 1])
             elif kind >= 0:
                 arrive(where(*args), wrecv.at[ARRIVALS.index(arrival(*args))])
+                if PIECES[kind][0] is not None:
+                    share(*args)
                 if kind == BIASED and args[1] == 0:
                     arrive(UB.at[wrap(z + sign * args[2], 8)], brecv.at[args[2] % 8])
             elif kind == SIB_D:
@@ -271,20 +285,18 @@
             send(block, block, sibs.at[1], sibr.at[16 + max(abs(dz) - 1, 0)], sibling)
         elif op == SHARE_D:
             h, dx, rp = args
-            there = ITEMS.index((h, -dx if dx in (-1, 1) else dx, rp))
             if rows_of(h, False) and dx in (1, 2):
                 block = D.at[0, 0, 0, :, pl.ds(0, rows_of(h, False)), pl.ds(0, 128)]
                 arrive(block, wrecv.at[ARRIVALS.index((2, h, dx, rp))])
             if rows_of(h, True):
                 block = D.at[0, 0, 0, 0, pl.ds(0, rows_of(h, True)), pl.ds(0, 128)]
                 arrive(block, wrecv.at[ARRIVALS.index((3, h, dx, 3 if rp else -4))])
-            send(
-                D.at[h, slot(dx), rp, :, :, pl.ds(0, 128)],
-                D.at[h, slot(-dx), rp, :, :, pl.ds(128, 128)],
-                sibs.at[0],
-                sibr.at[there],
-                sibling,
-            )
+            for kind, (half, _, _) in enumerate(PIECES):
+                if half == h:
+                    for dz in OFFSETS:
+                        own = dx == 0 and dz == 0
+                        if dz % 2 == rp and (own or arrival(kind, dx, dz)[0] != 0):
+                            share(kind, dx, dz)
         elif op == NORM:
             for copy in late:
                 copy.wait()

time: 82.2 us -> 82.2 us (level)
  no operation moved by 1% of the time
where the time goes in v5:
time: 82.2 us; the launch traced here: 81.9 us
  Pallas kernels  81 us (99%)
  local copies, waits for them, and re-layouts  0.97 us (1%)
    pallas_call x1, Pallas kernels, on_device(): pl.pallas_call(kernel, out_shape=pltpu.VMEM((128, 4096), BF16), in_specs=...  81 us

profile of v5, /device:TPU:1, one launch (start us, length us, event | category | flops | bytes accessed | tf_op | source)
XLA Modules:
  0.0 81.9 jit_solution(13007769604907959135)
XLA Ops:
  0.0 81.0 %shard_map.73 = bf16[128,4096]{1,0:T(8,128)(2,1)S(1)} custom-call(bf16[128,1024]{1,0:T(8,128)(2,1)} %tok.1, f32[1,1024]{1,0:T(1,128)} %bitcast.5, f32[1,1024]{1,0:T(1,128)} %bitcast.6, bf16[64,512]{1,0:T(8,128)(2,1)} %up.1, f32[1,512]{1,0:T(1,128)} %bitcast.7, bf16[512,256]{1,0:T(8,128)(2,1)} %down.1, f32[1,4096]{1,0:T(1,128)} %bitcast.4), custom_call_target="tpu_custom_call" | custom-call | tf_op jit(solution)/shard_map/pallas_call | solution.py:373
  81.0 1.0 %copy.9 = bf16[128,4096]{1,0:T(8,128)(2,1)} copy(bf16[128,4096]{1,0:T(8,128)(2,1)S(1)} %shard_map.73) | data formatting | bytes 2097152
